TPU v7x, 32 devices: a whole 2x2x4 slice. The times are simulated.
32 devices in a mesh: dp: 4 (over y, core), expert: 4 (over z), tensor: 2 (over x).
Axes of the slice: x: 2, y: 2, z: 4, core: 2. Of those that a mesh axis runs over, the one named last changes fastest.
Arguments:
- tokens: bfloat16 [256, 3072], P(('dp', 'expert')), may hold values from -45 to 45
- cotangent: bfloat16 [256, 3072], P(('dp', 'expert')), may hold values from -6 to 6
- gain: float32 [3072], replicated, may hold values from 0.5 to 1.5
- w_router: bfloat16 [3072, 4], replicated, may hold values from -0.109375 to 0.109375
- w_gate: bfloat16 [4, 3072, 9216], P('expert', None, 'tensor'), may hold values from -0.109375 to 0.109375
- w_up: bfloat16 [4, 3072, 9216], P('expert', None, 'tensor'), may hold values from -0.109375 to 0.109375
- w_down: bfloat16 [4, 9216, 3072], P('expert', 'tensor'), may hold values from -0.0625 to 0.0625
- expert_ids: int32 [256, 2], P(('dp', 'expert')), may hold values from 0 to 3, as said below
- slots: int32 [256, 2], P(('dp', 'expert')), may hold values from 0 to 7, as said below
Outputs:
- mixed: bfloat16 [256, 3072], P(('dp', 'expert'))
- grad_tokens: bfloat16 [256, 3072], P(('dp', 'expert'))
- grad_router: float32 [3072, 4], replicated
- grad_gain: float32 [3072], replicated
Inputs may be any that keep to these rules, and one draw needn't show every extreme that they name: `expert_ids`: within each aligned block of 16 rows (one group), every expert is named exactly 8 times, and a row's two ids differ. Within each aligned block of 16 rows, the choices naming one expert hold its slots 0 to 7, each once.
All inputs are finite; a program needn't handle non-finite values.
Results may differ from a plain program's by a relative error of at most 0.0095.
Values may be sent and summed in bfloat16 or wider, within the bound.
No kernel may reach another device: no remote copies, remote signals or barrier semaphores. Data moves between devices by JAX's collectives and lax.ppermute only.
A program may use at most 128 MiB of HBM per device.

v0:
```python
import jax
import jax.numpy as jnp
from jax import lax
from jax.sharding import PartitionSpec as P

epsilon = 1e-05


def pack_rows(select, values):
    return jnp.einsum("tcr,tcd->rd", select, values, preferred_element_type=jnp.float32).astype(
        jnp.bfloat16
    )


def repeat_blocks(packed, experts, copies):
    feature_width = packed.shape[1]
    blocks = packed.reshape(experts, 1, -1, feature_width)
    blocks = jnp.broadcast_to(blocks, (experts, copies, blocks.shape[2], feature_width))
    return blocks.reshape(experts * copies, -1, feature_width)


def to_experts(packed, experts, copies):
    arrived = lax.all_to_all(
        repeat_blocks(packed, experts, copies), "expert", split_axis=0, concat_axis=0, tiled=True
    )
    return arrived.reshape(-1, packed.shape[1])


def from_experts(partial_value, row_index, experts, copies):
    partial_value = lax.psum_scatter(
        partial_value.astype(jnp.bfloat16), "tensor", scatter_dimension=1, tiled=True
    ).astype(jnp.float32)
    feature_width = partial_value.shape[1]
    returned_rows = lax.all_to_all(
        partial_value.reshape(experts * copies, -1, feature_width),
        "expert",
        split_axis=0,
        concat_axis=0,
        tiled=True,
    )
    summed = jnp.sum(returned_rows.reshape(experts, copies, -1, feature_width), axis=1).reshape(
        -1, feature_width
    )
    picked = summed[row_index]
    picked = lax.all_gather(picked.astype(jnp.bfloat16), "tensor", axis=2, tiled=True).astype(
        picked.dtype
    )
    return picked


def shards(tokens, cotangent, gain, w_router, w_gate, w_up, w_down, expert_ids, slots):
    experts = w_router.shape[1]
    copies = lax.axis_size("expert") // experts
    token_count = tokens.shape[0]
    capacity = 2 * token_count // experts
    floats = tokens.astype(jnp.float32)
    inv_rms = lax.rsqrt(jnp.mean(floats * floats, axis=1, keepdims=True) + epsilon)
    normed = (floats * inv_rms * gain).astype(jnp.bfloat16)
    logits = jnp.dot(normed, w_router, preferred_element_type=jnp.float32)
    chosen_logits = jnp.take_along_axis(logits, expert_ids, axis=1)
    first_prob = jax.nn.sigmoid(chosen_logits[:, 0] - chosen_logits[:, 1])
    pair_probs = jnp.stack([first_prob, 1.0 - first_prob], axis=1)
    row_index = expert_ids * capacity + slots
    select = (
        row_index[:, :, None] == jnp.arange(experts * capacity, dtype=jnp.int32)[None, None, :]
    ).astype(jnp.bfloat16)
    feature_width = tokens.shape[1]
    inputs = to_experts(
        pack_rows(select, jnp.broadcast_to(normed[:, None, :], (token_count, 2, feature_width))),
        experts,
        copies,
    )
    gate_matrix = w_gate[0]
    up_matrix = w_up[0]
    down_matrix = w_down[0]
    gate_pre = jnp.dot(inputs, gate_matrix, preferred_element_type=jnp.float32)
    up_pre = jnp.dot(inputs, up_matrix, preferred_element_type=jnp.float32)
    activated = (jax.nn.silu(gate_pre) * up_pre).astype(jnp.bfloat16)
    chosen = from_experts(
        jnp.dot(activated, down_matrix, preferred_element_type=jnp.float32),
        row_index,
        experts,
        copies,
    )
    mixed = (floats + jnp.sum(pair_probs[:, :, None] * chosen, axis=1)).astype(jnp.bfloat16)
    upstream = cotangent.astype(jnp.float32)
    sent_grads = (pair_probs[:, :, None] * upstream[:, None, :]).astype(jnp.bfloat16)
    grad_outputs = to_experts(pack_rows(select, sent_grads), experts, copies)
    grad_act = jnp.dot(grad_outputs, down_matrix.T, preferred_element_type=jnp.float32)
    sigmoid_gate = jax.nn.sigmoid(gate_pre)
    grad_gate = (grad_act * up_pre * sigmoid_gate * (1.0 + gate_pre * (1.0 - sigmoid_gate))).astype(
        jnp.bfloat16
    )
    grad_up = (grad_act * jax.nn.silu(gate_pre)).astype(jnp.bfloat16)
    grad_inputs = jnp.dot(grad_gate, gate_matrix.T, preferred_element_type=jnp.float32) + jnp.dot(
        grad_up, up_matrix.T, preferred_element_type=jnp.float32
    )
    grad_mixture = jnp.sum(from_experts(grad_inputs, row_index, experts, copies), axis=1)
    grad_probs = jnp.sum(upstream[:, None, :] * chosen, axis=2)
    grad_first = first_prob * (1.0 - first_prob) * (grad_probs[:, 0] - grad_probs[:, 1])
    columns = jnp.arange(experts, dtype=jnp.int32)[None, :]
    grad_logits = grad_first[:, None] * (
        (expert_ids[:, 0:1] == columns).astype(jnp.float32)
        - (expert_ids[:, 1:2] == columns).astype(jnp.float32)
    )
    grad_normed = grad_mixture + jnp.dot(
        grad_logits, w_router.astype(jnp.float32).T, precision=lax.Precision.HIGHEST
    )
    router_part = jnp.dot(
        normed.astype(jnp.float32).T, grad_logits, precision=lax.Precision.HIGHEST
    )
    gain_part = jnp.sum(grad_normed * floats * inv_rms, axis=0)
    grad_router, grad_gain = lax.psum((router_part, gain_part), ("dp", "expert"))
    grad_scaled = grad_normed * gain
    cubed = inv_rms * inv_rms * inv_rms
    grad_tokens = (
        upstream
        + inv_rms * grad_scaled
        - floats * cubed * jnp.mean(grad_scaled * floats, axis=1, keepdims=True)
    ).astype(jnp.bfloat16)
    return (mixed, grad_tokens, grad_router, grad_gain)


def solution(mesh):
    return jax.shard_map(
        shards,
        mesh=mesh,
        in_specs=(
            P(("dp", "expert"), None),
            P(("dp", "expert"), None),
            P(),
            P(),
            P("expert", None, "tensor"),
            P("expert", None, "tensor"),
            P("expert", "tensor", None),
            P(("dp", "expert"), None),
            P(("dp", "expert"), None),
        ),
        out_specs=(P(("dp", "expert"), None), P(("dp", "expert"), None), P(), P()),
        check_vma=False,
    )
```

profile of v0, /device:TPU:0, one launch (start us, length us, event | category | flops | bytes accessed | tf_op | source)
XLA Modules:
  0.0 204.1 jit_solution(13842822642820997463)
XLA Ops:
  7.2 0.0 copy-start
  7.2 1.0 fusion.29
  8.2 0.7 compare_select_fusion
  8.9 1.0 fusion.31
  9.9 1.0 fusion.24
  10.9 6.3 %all-to-all-start = ((bf16[4,8,3072]{2,1,0:T(8,128)(2,1)}), bf16[4,8,3072]{2,1,0:T(8,128)(2,1)S(1)}, u32[]{:S(2)}, u32[]{:S(2)}) async-start(bf16[4,8,3072]{2,1,0:T(8,128)(2,1)} %fusion.24), calls=%async_computation | async-start | bytes 393216 | tf_op jit(solution)/shard_map/all_to_all | solution.py:23
  17.3 0.7 bitcast_or_fusion
  17.9 0.1 copy.39
  18.0 0.1 reshape.101
  18.1 0.0 copy-done
  18.1 0.1 fusion.59
  18.3 0.8 gather_fusion.2
  19.0 0.1 reshape.104
  19.1 0.1 copy.40
  19.2 0.7 and_select_fusion
  19.9 0.9 convert_element_type.70
  20.8 1.0 fusion.23
  21.8 2.9 %all-to-all-done = bf16[4,8,3072]{2,1,0:T(8,128)(2,1)S(1)} async-done(((bf16[4,8,3072]{2,1,0:T(8,128)(2,1)}), bf16[4,8,3072]{2,1,0:T(8,128)(2,1)S(1)}, u32[]{:S(2)}, u32[]{:S(2)}) %all-to-all-start) | async-done | bytes 196640 | tf_op jit(solution)/shard_map/all_to_all | solution.py:23
  24.8 3.4 %all-to-all-start.2 = ((bf16[4,8,3072]{2,1,0:T(8,128)(2,1)}), bf16[4,8,3072]{2,1,0:T(8,128)(2,1)S(1)}, u32[]{:S(2)}, u32[]{:S(2)}) async-start(bf16[4,8,3072]{2,1,0:T(8,128)(2,1)} %fusion.23), calls=%async_computation.3 | async-start | bytes 393216 | tf_op jit(solution)/shard_map/all_to_all | solution.py:23
  28.1 0.0 reduce-scatter.3.cloned.1.call-start
  28.2 11.5 %fusion.10 = f32[32,4608]{1,0:T(8,128)S(1)} fusion(bf16[1,3072,4608]{2,1,0:T(8,128)(2,1)} %param.13, bf16[4,8,3072]{2,1,0:T(8,128)(2,1)S(1)} %all-to-all-done), kind=kOutput, calls=%fused_computation.13 | convolution fusion | flops 905969664 | bytes 29097984 | tf_op jit(solution)/shard_map/dot_general | solution.py:76
  39.7 11.5 %fusion.6 = f32[32,4608]{1,0:T(8,128)S(1)} fusion(bf16[1,3072,4608]{2,1,0:T(8,128)(2,1)} %param.14, bf16[4,8,3072]{2,1,0:T(8,128)(2,1)S(1)} %all-to-all-done), kind=kOutput, calls=%fused_computation.9 | convolution fusion | flops 905969664 | bytes 29097984 | tf_op jit(solution)/shard_map/dot_general | solution.py:77
  51.2 12.3 %fusion.20 = bf16[32,3072]{1,0:T(8,128)(2,1)} fusion(bf16[1,4608,3072]{2,1,0:T(8,128)(2,1)} %param.15, f32[32,4608]{1,0:T(8,128)S(1)} %fusion.6, f32[32,4608]{1,0:T(8,128)S(1)} %fusion.10), kind=kOutput, calls=%fused_computation.21 | convolution fusion | flops 906952704 | bytes 29687808 | tf_op jit(solution)/shard_map/dot_general | solution.py:80
  63.6 0.0 reduce-scatter.3.cloned.1.call-update
  63.6 0.2 reduce-scatter.5.cloned.1.call-start
  63.8 0.0 all-to-all-done.2
  63.8 13.6 %fusion = f32[32,4608]{1,0:T(8,128)S(1)} fusion(bf16[1,4608,3072]{2,1,0:T(8,128)(2,1)} %param.15, bf16[4,8,3072]{2,1,0:T(8,128)(2,1)S(1)} %all-to-all-done.2), kind=kOutput, calls=%fused_computation.3 | convolution fusion | flops 905969664 | bytes 29097984 | tf_op jit(solution)/shard_map/dot_general | solution.py:89
  77.4 13.5 %fusion.4 = f32[32,3072]{1,0:T(8,128)S(1)} fusion(bf16[1,3072,4608]{2,1,0:T(8,128)(2,1)} %param.14, f32[32,4608]{1,0:T(8,128)S(1)} %fusion, f32[32,4608]{1,0:T(8,128)S(1)} %fusion.10), kind=kOutput, calls=%fused_computation.7 | convolution fusion | flops 906854400 | bytes 29884416 | tf_op jit(solution)/shard_map/dot_general | solution.py:95
  90.9 0.0 copy-start.4
  90.9 0.0 copy-start.1
  90.9 0.0 copy-start.3
  90.9 0.0 copy-start.2
  90.9 14.3 %fusion.15 = bf16[32,3072]{1,0:T(8,128)(2,1)} fusion(f32[32,3072]{1,0:T(8,128)S(1)} %fusion.4, bf16[1,3072,4608]{2,1,0:T(8,128)(2,1)} %param.13, f32[32,4608]{1,0:T(8,128)S(1)} %fusion.10, f32[32,4608]{1,0:T(8,128)S(1)} %fusion, f32[32,4608]{1,0:T(8,128)S(1)} %fusion.6), kind=kOutput, calls=%fused_computation.18 | convolution fusion | flops 907640832 | bytes 30670848 | tf_op jit(solution)/shard_map/dot_general | solution.py:95
  105.2 0.0 reduce-scatter.5.cloned.1.call-update
  105.2 0.0 reduce-scatter.3.cloned.1.call-done
  105.2 5.0 %all-to-all-start.1 = ((bf16[4,8,1536]{2,1,0:T(8,128)(2,1)}), bf16[4,8,1536]{2,1,0:T(8,128)(2,1)S(1)}, u32[]{:S(2)}, u32[]{:S(2)}) async-start(bf16[4,8,1536]{2,1,0:T(8,128)(2,1)} %bitcast.72), calls=%async_computation.2 | async-start | bytes 196608 | tf_op jit(solution)/shard_map/all_to_all | solution.py:34
  110.3 0.0 copy-done.4
  110.3 0.1 copy.41
  110.4 0.1 reshape.87
  110.5 7.3 %reduce-scatter.5.cloned.1.call-done = bf16[32,1536]{1,0:T(8,128)(2,1)} async-done(((bf16[32,3072]{1,0:T(8,128)(2,1)}), bf16[32,1536]{1,0:T(8,128)(2,1)}) %reduce-scatter.5.cloned.1.call-update) | async-done | bytes 98320 | tf_op jit(solution)/shard_map/reduce_scatter | solution.py:30
  117.8 0.0 all-to-all-done.1
  117.8 4.6 %all-to-all-start.3 = ((bf16[4,8,1536]{2,1,0:T(8,128)(2,1)}), bf16[4,8,1536]{2,1,0:T(8,128)(2,1)S(1)}, u32[]{:S(2)}, u32[]{:S(2)}) async-start(bf16[4,8,1536]{2,1,0:T(8,128)(2,1)} %bitcast.71), calls=%async_computation.5 | async-start | bytes 196608 | tf_op jit(solution)/shard_map/all_to_all | solution.py:34
  122.4 0.6 gather_fusion
  123.1 5.3 %all_gather.6 = bf16[16,2,3072]{2,0,1:T(8,128)(2,1)S(1)} all-gather(bf16[16,2,1536]{2,0,1:T(8,128)(2,1)S(1)} %copy.42), channel_id=1, replica_groups=mesh['dp'=4,'expert'=4,'tensor'=2] {'tensor'}, dimensions={2}, use_global_device_ids=true | all-gather | bytes 294912 | tf_op jit(solution)/shard_map/all_gather | solution.py:45
  128.4 0.1 fusion.27
  128.5 0.0 all-to-all-done.3
  128.5 0.6 gather_fusion.1
  129.2 5.3 %all_gather.7 = bf16[16,2,3072]{2,1,0:T(2,128)(2,1)S(1)} all-gather(bf16[16,2,1536]{2,1,0:T(2,128)(2,1)S(1)} %reshape.112), channel_id=1, replica_groups=mesh['dp'=4,'expert'=4,'tensor'=2] {'tensor'}, dimensions={2}, use_global_device_ids=true | all-gather | bytes 294912 | tf_op jit(solution)/shard_map/all_gather | solution.py:45
  134.5 0.5 convert_reduce_fusion
  135.0 0.3 fusion.47
  135.4 0.0 copy-done.1
  135.4 0.0 copy-done.3
  135.4 0.5 fusion.38
  135.8 60.6 %all-reduce = (f32[3072,4]{0,1:T(4,128)}, f32[3072]{0:T(1024)}) all-reduce(f32[3072,4]{0,1:T(4,128)S(1)} %fusion.47, f32[3072]{0:T(1024)S(1)} %get-tuple-element.4), channel_id=1, replica_groups=mesh['dp'=4,'expert'=4,'tensor'=2] {'dp','expert'}, use_global_device_ids=true, to_apply=%region_7.8 | all-reduce | flops 15360 | bytes 122880 | tf_op jit(solution)/shard_map/psum | solution.py:113
  196.5 0.0 copy-done.2
  196.5 0.8 fusion.35
  (10 shorter events, 0.2 us)
Async XLA Ops:
  7.2 11.0 %copy-start = (bf16[3072,4]{0,1:T(4,128)(2,1)S(1)}, bf16[3072,4]{0,1:T(4,128)(2,1)}, u32[]{:S(2)}) copy-start(bf16[3072,4]{0,1:T(4,128)(2,1)} %param.12) | copy-start | bytes 73732
  10.9 13.9 %all-to-all-start = ((bf16[4,8,3072]{2,1,0:T(8,128)(2,1)}), bf16[4,8,3072]{2,1,0:T(8,128)(2,1)S(1)}, u32[]{:S(2)}, u32[]{:S(2)}) async-start(bf16[4,8,3072]{2,1,0:T(8,128)(2,1)} %fusion.24), calls=%async_computation | async-start | bytes 393216 | tf_op jit(solution)/shard_map/all_to_all | solution.py:23
  24.8 39.0 %all-to-all-start.2 = ((bf16[4,8,3072]{2,1,0:T(8,128)(2,1)}), bf16[4,8,3072]{2,1,0:T(8,128)(2,1)S(1)}, u32[]{:S(2)}, u32[]{:S(2)}) async-start(bf16[4,8,3072]{2,1,0:T(8,128)(2,1)} %fusion.23), calls=%async_computation.3 | async-start | bytes 393216 | tf_op jit(solution)/shard_map/all_to_all | solution.py:23
  28.1 77.1 %reduce-scatter.3.cloned.1.call-start = ((), (), s32[]{:S(2)}) async-start(), calls=%async_computation.6 | async-start | bytes 294912 | tf_op jit(solution)/shard_map/reduce_scatter | solution.py:30
  63.6 54.2 %reduce-scatter.5.cloned.1.call-start = ((), (), s32[]{:S(2)}) async-start(), calls=%async_computation.7 | async-start | bytes 294912 | tf_op jit(solution)/shard_map/reduce_scatter | solution.py:30
  90.9 19.4 %copy-start.4 = (s32[16,2]{0,1:T(2,128)S(1)}, s32[16,2]{0,1:T(2,128)}, u32[]{:S(2)}) copy-start(s32[16,2]{0,1:T(2,128)} %param.16) | copy-start | bytes 388
  90.9 44.5 %copy-start.1 = (bf16[16,3072]{1,0:T(8,128)(2,1)S(1)}, bf16[16,3072]{1,0:T(8,128)(2,1)}, u32[]{:S(2)}) copy-start(bf16[16,3072]{1,0:T(8,128)(2,1)} %param.9) | copy-start | bytes 294916
  90.9 44.5 %copy-start.3 = (f32[3072]{0:T(1024)S(1)}, f32[3072]{0:T(1024)}, u32[]{:S(2)}) copy-start(f32[3072]{0:T(1024)} %param.11) | copy-start | bytes 36868
  90.9 105.5 %copy-start.2 = (bf16[16,3072]{1,0:T(8,128)(2,1)S(1)}, bf16[16,3072]{1,0:T(8,128)(2,1)}, u32[]{:S(2)}) copy-start(bf16[16,3072]{1,0:T(8,128)(2,1)} %param.10) | copy-start | bytes 294916
  105.2 12.5 %all-to-all-start.1 = ((bf16[4,8,1536]{2,1,0:T(8,128)(2,1)}), bf16[4,8,1536]{2,1,0:T(8,128)(2,1)S(1)}, u32[]{:S(2)}, u32[]{:S(2)}) async-start(bf16[4,8,1536]{2,1,0:T(8,128)(2,1)} %bitcast.72), calls=%async_computation.2 | async-start | bytes 196608 | tf_op jit(solution)/shard_map/all_to_all | solution.py:34
  117.8 10.8 %all-to-all-start.3 = ((bf16[4,8,1536]{2,1,0:T(8,128)(2,1)}), bf16[4,8,1536]{2,1,0:T(8,128)(2,1)S(1)}, u32[]{:S(2)}, u32[]{:S(2)}) async-start(bf16[4,8,1536]{2,1,0:T(8,128)(2,1)} %bitcast.71), calls=%async_computation.5 | async-start | bytes 196608 | tf_op jit(solution)/shard_map/all_to_all | solution.py:34
Sparse Core Ops, SparseCore 0:
  63.7 12.3 reduce-scatter.2
  105.3 12.3 reduce-scatter.4
where the time goes:
time: 205 us; the launch traced here: 204 us
  matrix products  79.6 us (39%)
  blocking collectives  71.2 us (35%)
  starting transfers between devices  19.6 us (10%)
  between operations  14.2 us (7%)
  waiting for transfers between devices  10.3 us (5%)
  other arithmetic  6.49 us (3%)
  local copies, waits for them, and re-layouts  2.68 us (1%)
    psum x1, blocking collectives, shards(): lax.psum((router_part, gain_part), ('dp', 'expert'))  60.6 us
    dot_general x1, matrix products, shards(): jnp.dot(grad_gate, gate_matrix.T, preferred_element_type=jnp.float32)  14.3 us
    dot_general x1, matrix products, shards(): jnp.dot(grad_outputs, down_matrix.T, preferred_element_type=jnp.float32)  13.6 us
    dot_general x1, matrix products, shards(): jnp.dot(grad_up, up_matrix.T, preferred_element_type=jnp.float32)  13.5 us
    dot_general x1, matrix products, shards(): jnp.dot(activated, down_matrix, preferred_element_type=jnp.float32)  12.3 us
    dot_general x1, matrix products, shards(): gate_pre = jnp.dot(inputs, gate_matrix, preferred_element_type=jnp.float32)  11.5 us
    dot_general x1, matrix products, shards(): up_pre = jnp.dot(inputs, up_matrix, preferred_element_type=jnp.float32)  11.5 us
    all_gather x2, blocking collectives, from_experts(): lax.all_gather(picked.astype(jnp.bfloat16), 'tensor', axis=2, tiled=True)  10.6 us
  transfers between devices with their start and end apart: 6, of which 2 were waited for; matrix products, arithmetic and copies ran while one was open for 40% of the time, Pallas kernels for 0%

commit v1 on v0

v1 whole, which is shorter than its diff:
```python
import functools

import jax
import jax.numpy as jnp
from jax import lax
from jax.experimental import pallas as pl
from jax.experimental.pallas import tpu as pltpu
from jax.sharding import PartitionSpec as P

epsilon = 1e-05
MIB = 1 << 20
VMEM = pl.BlockSpec(memory_space=pltpu.VMEM)
SMEM = pl.BlockSpec(memory_space=pltpu.SMEM)
HBM = pl.BlockSpec(memory_space=pltpu.HBM)
NN = (((1,), (0,)), ((), ()))
NT = (((1,), (1,)), ((), ()))
TN = (((0,), (0,)), ((), ()))


def mm(a, b, dims):
    return lax.dot_general(a, b, dims, preferred_element_type=jnp.float32)


def shape(dims, dtype):
    return jax.ShapeDtypeStruct(dims, dtype)


def call(body, ins, in_specs, outs, scratch=(), limit=8, flops=0, moved=0):
    return pl.pallas_call(
        body,
        in_specs=in_specs,
        out_specs=[VMEM] * len(outs),
        out_shape=outs,
        scratch_shapes=scratch,
        compiler_params=pltpu.CompilerParams(vmem_limit_bytes=limit * MIB),
        cost_estimate=pl.CostEstimate(flops=flops, bytes_accessed=moved, transcendentals=0),
    )(*ins)


def piece(size):
    for width in (256, 128):
        if size % width == 0:
            return width
    return size


def one_hot(index_ref, column, rows):
    places = lax.broadcasted_iota(jnp.int32, (index_ref.shape[0], rows), 1)
    return index_ref[:, column : column + 1] == places


def pack_tokens(index_ref, tokens_ref, *refs):
    rows = len(refs) * refs[0].shape[0]
    select = (one_hot(index_ref, 0, rows) | one_hot(index_ref, 1, rows)).astype(jnp.bfloat16)
    split(mm(select, tokens_ref[...], TN), refs)


def route_grads(index_ref, ids_ref, tokens_ref, cotangent_ref, gain_ref, router_ref, *refs):
    *rows_refs, probs_ref, inv_ref, normed_ref = refs
    rows = len(rows_refs) * rows_refs[0].shape[0]
    floats = tokens_ref[...].astype(jnp.float32)
    inv = lax.rsqrt(jnp.mean(floats * floats, axis=1, keepdims=True) + epsilon)
    normed = (floats * inv * gain_ref[...]).astype(jnp.bfloat16)
    logits = mm(normed, router_ref[...], NN)
    experts = logits.shape[1]
    first = jnp.sum(jnp.where(one_hot(ids_ref, 0, experts), logits, 0.0), axis=1, keepdims=True)
    second = jnp.sum(jnp.where(one_hot(ids_ref, 1, experts), logits, 0.0), axis=1, keepdims=True)
    prob = jax.nn.sigmoid(first - second)
    upstream = cotangent_ref[...].astype(jnp.float32)
    sent_first = (prob * upstream).astype(jnp.bfloat16)
    sent_second = ((1.0 - prob) * upstream).astype(jnp.bfloat16)
    packed = mm(one_hot(index_ref, 0, rows).astype(jnp.bfloat16), sent_first, TN)
    packed += mm(one_hot(index_ref, 1, rows).astype(jnp.bfloat16), sent_second, TN)
    split(packed, rows_refs)
    probs_ref[...] = jnp.broadcast_to(prob, probs_ref.shape)
    inv_ref[...] = jnp.broadcast_to(inv, inv_ref.shape)
    normed_ref[...] = normed


def stack(refs):
    return jnp.concatenate([ref[...].astype(jnp.float32) for ref in refs], axis=0)


def forward(count, part_ref, *refs):
    tokens_refs = refs[:count]
    gain_ref, gate_ref, up_ref = refs[count : count + 3]
    act_ref, slope_ref, silu_ref, inv_ref, gate_here, up_here, sems = refs[count + 3 :]
    inner = act_ref.shape[1]
    width = piece(inner)
    copies = []
    for step in range(inner // width):
        here = pl.ds(step * width, width)
        there = pl.ds(pl.multiple_of(part_ref[0] * inner + step * width, width), width)
        pair = [
            pltpu.make_async_copy(ref.at[:, there], out.at[:, here], sems.at[2 * step + side])
            for side, (ref, out) in enumerate(((gate_ref, gate_here), (up_ref, up_here)))
        ]
        for copy in pair:
            copy.start()
        copies.append(pair)
    floats = stack(tokens_refs)
    inv = lax.rsqrt(jnp.mean(floats * floats, axis=1, keepdims=True) + epsilon)
    inv_ref[...] = jnp.broadcast_to(inv, inv_ref.shape)
    normed = (floats * inv * gain_ref[...]).astype(jnp.bfloat16)
    for step in range(inner // width):
        span = pl.ds(step * width, width)
        copies[step][0].wait()
        gate = mm(normed, gate_here[:, span], NN)
        copies[step][1].wait()
        up = mm(normed, up_here[:, span], NN)
        sigmoid = jax.nn.sigmoid(gate)
        silu = gate * sigmoid
        act_ref[:, span] = (silu * up).astype(jnp.bfloat16)
        slope_ref[span, :] = (up * sigmoid * (1.0 + gate * (1.0 - sigmoid))).T
        silu_ref[span, :] = silu.T


def middle(count, part_ref, *refs):
    act_ref, slope_ref, silu_ref, down_ref = refs[:4]
    grads_refs = refs[4 : 4 + count]
    *value_refs, gate_ref, up_ref, total_ref, down_here, sems = refs[4 + count :]
    inner = down_here.shape[0]
    height = piece(inner)
    copies = []
    for step in range(inner // height):
        there = pl.ds(pl.multiple_of(part_ref[0] * inner + step * height, height), height)
        copy = pltpu.make_async_copy(
            down_ref.at[there, :], down_here.at[pl.ds(step * height, height), :], sems.at[step]
        )
        copy.start()
        copies.append(copy)
    grads = stack(grads_refs).astype(jnp.bfloat16)
    for step in range(inner // height):
        span = pl.ds(step * height, height)
        copies[step].wait()
        value = mm(act_ref[:, span], down_here[span, :], NN)
        total_ref[...] = value if step == 0 else total_ref[...] + value
        grad_act = mm(down_here[span, :], grads, NT)
        gate_ref[span, :] = (grad_act * slope_ref[span, :]).astype(jnp.bfloat16)
        up_ref[span, :] = (grad_act * silu_ref[span, :]).astype(jnp.bfloat16)
    rows = value_refs[0].shape[0]
    for part, value_ref in enumerate(value_refs):
        value_ref[...] = total_ref[pl.ds(part * rows, rows), :].astype(value_ref.dtype)


def backward(count, *refs):
    gate_grad_ref, up_grad_ref, gate_ref, up_ref, inv_ref = refs[:5]
    tokens_refs = refs[5 : 5 + count]
    *value_refs, gain_ref = refs[5 + count :]
    rows = value_refs[0].shape[0]
    height = piece(gate_ref.shape[0])
    for start in range(0, gate_ref.shape[0], height):
        span = pl.ds(start, height)
        back = mm(gate_ref[span, :], gate_grad_ref[...], NN) + mm(up_ref[span, :], up_grad_ref[...], NN)
        back = back.T
        for part, value_ref in enumerate(value_refs):
            value_ref[:, span] = back[part * rows : (part + 1) * rows].astype(value_ref.dtype)
        floats = jnp.concatenate([ref[:, span].astype(jnp.float32) for ref in tokens_refs], axis=0)
        gain_ref[:, span] = jnp.sum(back * (floats * inv_ref[:, :1]), axis=0, keepdims=True)


def split(value, refs):
    rows = refs[0].shape[0]
    for place, ref in enumerate(refs):
        ref[...] = value[place * rows : (place + 1) * rows].astype(ref.dtype)


def add_pair(own_ref, other_ref, *refs):
    split(own_ref[...] + other_ref[...].astype(jnp.float32), refs)


def mix_rows(index_ref, probs_ref, cotangent_ref, *refs):
    *rows_refs, mix_ref, score_ref = refs
    rows = stack(rows_refs).astype(jnp.bfloat16)
    first = mm(one_hot(index_ref, 0, rows.shape[0]).astype(jnp.bfloat16), rows, NN)
    second = mm(one_hot(index_ref, 1, rows.shape[0]).astype(jnp.bfloat16), rows, NN)
    prob = probs_ref[:, :1]
    mix_ref[...] = (prob * first + (1.0 - prob) * second).astype(jnp.bfloat16)
    score = jnp.sum(cotangent_ref[...].astype(jnp.float32) * (first - second), axis=1, keepdims=True)
    score_ref[...] = jnp.broadcast_to(score, score_ref.shape)


def sum_rows(index_ref, *refs):
    *rows_refs, out_ref = refs
    rows = stack(rows_refs).astype(jnp.bfloat16)
    select = (one_hot(index_ref, 0, rows.shape[0]) | one_hot(index_ref, 1, rows.shape[0])).astype(jnp.bfloat16)
    out_ref[...] = mm(select, rows, NN).astype(jnp.bfloat16)


def finish_values(share, ids_ref, tokens_ref, mine_ref, other_ref, score_ref, other_score_ref, probs_ref, inv_ref, normed_ref, router_ref, mixed_ref, term_ref, parts_ref):
    floats = tokens_ref[...].astype(jnp.float32)
    mix = mine_ref[...].astype(jnp.float32) + other_ref[...].astype(jnp.float32)
    mixed_ref[...] = (floats + mix).astype(jnp.bfloat16)
    prob = probs_ref[:, :1]
    grad_first = prob * (1.0 - prob) * (score_ref[:, :1] + other_score_ref[:, :1])
    experts = router_ref.shape[0]
    grad_logits = jnp.where(one_hot(ids_ref, 0, experts), grad_first, 0.0)
    grad_logits -= jnp.where(one_hot(ids_ref, 1, experts), grad_first, 0.0)
    normed = normed_ref[...].astype(jnp.float32)
    term = jnp.zeros(floats.shape, jnp.float32)
    for expert in range(experts):
        column = grad_logits[:, expert : expert + 1]
        term += column * router_ref[expert : expert + 1, :].astype(jnp.float32)
        parts_ref[expert : expert + 1, :] = share * jnp.sum(column * normed, axis=0, keepdims=True)
    term_ref[...] = term
    local = jnp.sum(term * floats * inv_ref[:, :1], axis=0, keepdims=True)
    parts_ref[experts : experts + 1, :] = share * local


def finish_grads(tokens_ref, cotangent_ref, gain_ref, mine_ref, other_ref, term_ref, inv_ref, out_ref):
    floats = tokens_ref[...].astype(jnp.float32)
    inv = inv_ref[:, :1]
    grad_normed = mine_ref[...].astype(jnp.float32) + other_ref[...].astype(jnp.float32) + term_ref[...]
    grad_scaled = grad_normed * gain_ref[...]
    mean = jnp.mean(grad_scaled * floats, axis=1, keepdims=True)
    out_ref[...] = (
        cotangent_ref[...].astype(jnp.float32) + inv * grad_scaled - floats * (inv * inv * inv) * mean
    ).astype(jnp.bfloat16)


def swap(value, axis):
    size = lax.axis_size(axis)
    return lax.ppermute(value, axis, [(i, i ^ 1) for i in range(size)])


def sum_over(value, axis):
    size = lax.axis_size(axis)
    if size == 1:
        return value, jnp.zeros_like(value)
    if size == 2:
        return value, swap(value, axis)
    total = lax.psum(value.astype(jnp.float32), axis)
    return total.astype(value.dtype), jnp.zeros_like(value)


def trade(blocks, copies):
    if len(blocks) > 1:
        size = len(blocks)
        pairs = [[(i, i ^ step) for i in range(size)] for step in range(size)]
        return [blocks[0]] + [lax.ppermute(blocks[step], "expert", pairs[step]) for step in range(1, size)]
    size = lax.axis_size("expert")
    width = blocks[0].shape[1]
    if copies:
        experts = size // copies
        rows = blocks[0].reshape(experts, 1, -1, width)
        rows = jnp.broadcast_to(rows, (experts, copies) + rows.shape[2:])
    else:
        rows = blocks[0]
    rows = rows.reshape(size, -1, width)
    return [lax.all_to_all(rows, "expert", split_axis=0, concat_axis=0, tiled=True).reshape(-1, width)]


def bring_back(blocks, copies, experts):
    back = trade(blocks, 0)
    if copies > 1:
        rows = back[0].reshape(experts, copies, -1, back[0].shape[1]).astype(jnp.float32)
        back = [jnp.sum(rows, axis=1).reshape(-1, rows.shape[3]).astype(jnp.bfloat16)]
    return back


def all_sum(value, axes):
    count = 1
    for axis in axes:
        count *= lax.axis_size(axis)
    if value.size % count:
        return lax.psum(value, axes)
    blocks = value.reshape(count, -1)
    mine = lax.all_to_all(blocks, axes, split_axis=0, concat_axis=0, tiled=True)
    total = jnp.sum(mine, axis=0, keepdims=True)
    spread = jnp.broadcast_to(total, blocks.shape)
    return lax.all_to_all(spread, axes, split_axis=0, concat_axis=0, tiled=True).reshape(value.shape)


def layer(tokens, cotangent, gain, w_router, w_gate, w_up, w_down, expert_ids, slots):
    experts = w_router.shape[1]
    axis = lax.axis_size("expert")
    copies = axis // experts
    token_count, width = tokens.shape
    rows = 2 * token_count
    capacity = rows // experts
    hidden = w_gate.shape[2]
    parts = 2 if lax.axis_size("dp") % 2 == 0 and hidden % 256 == 0 else 1
    inner = hidden // parts
    paired = copies == 1 and axis in (2, 4, 8) and capacity % 8 == 0
    owner = expert_ids ^ lax.axis_index("expert") if paired else expert_ids
    index = owner * capacity + slots
    part = (lax.axis_index("dp") % parts).astype(jnp.int32).reshape(1)
    gain_row = gain.reshape(1, width)
    bf16, f32 = jnp.bfloat16, jnp.float32
    sends = [shape((capacity, width), bf16)] * experts if paired else [shape((rows, width), bf16)]
    count = axis * capacity
    all_rows = parts * count
    backs_shape = [shape((capacity, width), bf16)] * experts if paired else [shape((count, width), bf16)]

    gate_there, up_there, down_there = (
        pltpu.with_memory_space_constraint(w[0], pltpu.HBM) for w in (w_gate, w_up, w_down)
    )
    packed = call(pack_tokens, (index, tokens), [VMEM] * 2, sends)
    inputs = trade(packed, copies)
    *sent, probs, inv, normed = call(
        route_grads,
        (index, expert_ids, tokens, cotangent, gain_row, w_router),
        [VMEM] * 6,
        sends + [shape((token_count, 128), f32), shape((token_count, 128), f32), shape((token_count, width), bf16)],
    )
    grads = trade(sent, copies)
    if parts == 2:
        inputs = inputs + [swap(block, "dp") for block in inputs]
        grads = grads + [swap(block, "dp") for block in grads]
    pieces = len(inputs)
    steps = inner // piece(inner)
    act, slope, silu, inv_rows, gate_here, up_here = call(
        functools.partial(forward, pieces),
        (part, *inputs, gain_row, gate_there, up_there),
        [SMEM] + [VMEM] * (pieces + 1) + [HBM] * 2,
        [
            shape((all_rows, inner), bf16),
            shape((inner, all_rows), f32),
            shape((inner, all_rows), f32),
            shape((all_rows, 128), f32),
            pltpu.VMEM((width, inner), bf16),
            pltpu.VMEM((width, inner), bf16),
        ],
        [pltpu.SemaphoreType.DMA((2 * steps,))],
        flops=4 * all_rows * width * inner,
        moved=4 * width * inner,
    )
    value_shapes = [shape((count, width), f32)] + [shape((count, width), bf16)] * (parts - 1)
    *values, gate_grad, up_grad = call(
        functools.partial(middle, pieces),
        (part, act, slope, silu, down_there, *grads),
        [SMEM] + [VMEM] * 3 + [HBM] + [VMEM] * pieces,
        value_shapes + [shape((inner, all_rows), bf16)] * 2,
        [pltpu.VMEM((all_rows, width), f32), pltpu.VMEM((inner, width), bf16), pltpu.SemaphoreType.DMA((steps,))],
        limit=20,
        flops=4 * all_rows * width * inner,
        moved=2 * width * inner,
    )
    gate_here, up_here = (pltpu.with_memory_space_constraint(w, pltpu.VMEM) for w in (gate_here, up_here))
    *backs, gain_part = call(
        functools.partial(backward, pieces),
        (gate_grad, up_grad, gate_here, up_here, inv_rows, *inputs),
        [VMEM] * (5 + pieces),
        value_shapes + [shape((1, width), f32)],
        flops=4 * all_rows * width * inner,
        moved=4 * width * inner,
    )

    def home(pieces):
        if parts == 2:
            mine = call(add_pair, (pieces[0], swap(pieces[1], "dp")), [VMEM] * 2, backs_shape)
        else:
            mine = [pieces[0].astype(bf16)] if not paired else [
                pieces[0][i * capacity : (i + 1) * capacity].astype(bf16) for i in range(experts)
            ]
        return bring_back(mine, copies, experts)

    value_rows = home(values)
    mix, score = call(
        mix_rows,
        (index, probs, cotangent, *value_rows),
        [VMEM] * (3 + len(value_rows)),
        [shape((token_count, width), bf16), shape((token_count, 128), f32)],
    )
    mix, other_mix = sum_over(mix, "tensor")
    score, other_score = sum_over(score, "tensor")
    mixed, term, local = call(
        functools.partial(finish_values, 1.0 / lax.axis_size("tensor")),
        (expert_ids, tokens, mix, other_mix, score, other_score, probs, inv, normed, w_router.T),
        [VMEM] * 10,
        [shape((token_count, width), bf16), shape((token_count, width), f32), shape((experts + 1, width), f32)],
    )
    back_rows = home(backs)
    (back,) = call(sum_rows, (index, *back_rows), [VMEM] * (1 + len(back_rows)), [shape((token_count, width), bf16)])
    back, other_back = sum_over(back, "tensor")
    (grad_tokens,) = call(
        finish_grads,
        (tokens, cotangent, gain_row, back, other_back, term, inv),
        [VMEM] * 7,
        [shape((token_count, width), bf16)],
    )
    local = jnp.concatenate([local[:experts], local[experts:] + gain_part], axis=0)
    total = all_sum(local, ("dp", "expert", "tensor"))
    return (mixed, grad_tokens, total[:experts].T, total[experts])


def solution(mesh):
    return jax.shard_map(
        layer,
        mesh=mesh,
        in_specs=(
            P(("dp", "expert"), None),
            P(("dp", "expert"), None),
            P(),
            P(),
            P("expert", None, "tensor"),
            P("expert", None, "tensor"),
            P("expert", "tensor", None),
            P(("dp", "expert"), None),
            P(("dp", "expert"), None),
        ),
        out_specs=(P(("dp", "expert"), None), P(("dp", "expert"), None), P(), P()),
        check_vma=False,
    )
```

time: 205 us -> 107 us (0.52)
  matrix products: 79.6 us -> 0 us
  blocking collectives: 71.2 us -> 0 us
  Pallas kernels: 0 us -> 36.2 us
  local copies, waits for them, and re-layouts: 2.68 us -> 19.6 us
  between operations: 14.2 us -> 0.9 us
  starting transfers between devices: 19.6 us -> 32.1 us
  waiting for transfers between devices: 10.3 us -> 17.4 us
  other arithmetic: 6.49 us -> 0.28 us
    dot_general x11 -> x0, matrix products: 79.6 us -> none  [the longest x1 14.3 us: shards(): jnp.dot(grad_gate, gate_matrix.T, preferred_element_type=jnp.float32)]
    psum x1 -> x0, blocking collectives: 60.6 us -> none  [shards(): lax.psum((router_part, gain_part), ('dp', 'expert'))]
    pallas_call x0 -> x11, Pallas kernels: none -> 36.2 us  [call(): pl.pallas_call(body, in_specs=in_specs, out_specs=[VMEM] * len(outs), out...]
    ppermute x0 -> x25, starting transfers between devices: none -> 24.8 us  [the longest x12 19.1 us: trade(): lax.ppermute(blocks[step], 'expert', pairs[step])]
    unnamed x10 -> x25, local copies, waits for them, and re-layouts: 0.03 us -> 16.8 us
    ppermute x0 -> x25, waiting for transfers between devices: none -> 13.8 us  [the longest x12 9.01 us: trade(): lax.ppermute(blocks[step], 'expert', pairs[step])]
    all_to_all x4 -> x2, starting transfers between devices: 19.3 us -> 7.33 us  [the longest x1 4.42 us: all_sum(): mine = lax.all_to_all(blocks, axes, split_axis=0, concat_axis=0, tiled=True)]
    all_gather x2 -> x0, blocking collectives: 10.6 us -> none  [from_experts(): lax.all_gather(picked.astype(jnp.bfloat16), 'tensor', axis=2, tiled=True)]
  transfers between devices with their start and end apart: 6 -> 27, of which waited for: 2 -> 9; matrix products, arithmetic and copies ran while one was open for 40% -> 2% of each run, Pallas kernels for 0% -> 22%
where the time goes in v1:
time: 107 us
  Pallas kernels  36.2 us (34%)
  starting transfers between devices  32.1 us (30%)
  local copies, waits for them, and re-layouts  19.6 us (18%)
  waiting for transfers between devices  17.4 us (16%)
    pallas_call x11, Pallas kernels, call(): pl.pallas_call(body, in_specs=in_specs, out_specs=[VMEM] * len(outs), out...  36.2 us
    ppermute x12, starting transfers between devices, trade(): lax.ppermute(blocks[step], 'expert', pairs[step])  19.1 us
    unnamed x25, local copies, waits for them, and re-layouts  16.8 us
    ppermute x12, waiting for transfers between devices, trade(): lax.ppermute(blocks[step], 'expert', pairs[step])  9.01 us
    ppermute x13, starting transfers between devices, swap(): return lax.ppermute(value, axis, [(i, i ^ 1) for i in range(size)])  5.74 us
    ppermute x13, waiting for transfers between devices, swap(): return lax.ppermute(value, axis, [(i, i ^ 1) for i in range(size)])  4.74 us
    all_to_all x1, starting transfers between devices, all_sum(): mine = lax.all_to_all(blocks, axes, split_axis=0, concat_axis=0, tiled=True)  4.42 us
    all_to_all x1, waiting for transfers between devices, all_sum(): mine = lax.all_to_all(blocks, axes, split_axis=0, concat_axis=0, tiled=True)  2.93 us
  transfers between devices with their start and end apart: 27, of which 9 were waited for; matrix products, arithmetic and copies ran while one was open for 2% of the time, Pallas kernels for 22%

profile of v1, /device:TPU:0, one launch (start us, length us, event | category | flops | bytes accessed | tf_op | source)
XLA Modules:
  0.0 106.5 jit_solution(18311071137134045757)
XLA Ops:
  0.6 0.8 copy.22.ids_ref
  1.4 0.8 copy.19
  2.2 0.9 copy-done.2
  3.0 0.3 shard_map.121
  3.3 3.1 %collective-permute-start = (bf16[8,3072]{1,0:T(8,128)(2,1)S(1)}, bf16[8,3072]{1,0:T(8,128)(2,1)S(1)}, u32[]{:S(2)}, u32[]{:S(2)}) collective-permute-start(bf16[8,3072]{1,0:T(8,128)(2,1)S(1)} %get-tuple-element.43), channel_id=1, source_target_pairs={{0,2},{2,0},{4,6},{6,4},{1,3},{3,1},{5,7},{7,5},{8,10},{10,8},{12,... | collective-permute-start | bytes 147464 | tf_op jit(solution)/shard_map/ppermute | solution.py:240
  6.5 2.6 %collective-permute-start.1 = (bf16[8,3072]{1,0:T(8,128)(2,1)S(1)}, bf16[8,3072]{1,0:T(8,128)(2,1)S(1)}, u32[]{:S(2)}, u32[]{:S(2)}) collective-permute-start(bf16[8,3072]{1,0:T(8,128)(2,1)S(1)} %get-tuple-element.44), channel_id=1, source_target_pairs={{0,4},{2,6},{4,0},{6,2},{1,5},{3,7},{5,1},{7,3},{8,12},{10,14},{12... | collective-permute-start | bytes 147464 | tf_op jit(solution)/shard_map/ppermute | solution.py:240
  9.1 1.2 %copy.21.router_ref = bf16[3072,4]{1,0:T(8,128)(2,1)S(1)} copy(bf16[3072,4]{0,1:T(4,128)(2,1)} %param.12) | data formatting | bytes 49152 | tf_op args[3]
  10.2 0.9 copy-done.3
  11.1 0.9 copy-done.5
  12.0 0.7 copy-done.7
  12.7 0.6 shard_map.120
  13.4 1.0 collective-permute-start.7
  14.3 3.5 %collective-permute-start.8 = (bf16[8,3072]{1,0:T(8,128)(2,1)S(1)}, bf16[8,3072]{1,0:T(8,128)(2,1)S(1)}, u32[]{:S(2)}, u32[]{:S(2)}) collective-permute-start(bf16[8,3072]{1,0:T(8,128)(2,1)S(1)} %get-tuple-element.51), channel_id=1, source_target_pairs={{0,4},{2,6},{4,0},{6,2},{1,5},{3,7},{5,1},{7,3},{8,12},{10,14},{12... | collective-permute-start | bytes 147464 | tf_op jit(solution)/shard_map/ppermute | solution.py:240
  17.8 0.0 collective-permute-start.9
  17.8 0.0 collective-permute-done.2.refs_3_.refs_8_
  17.8 0.1 collective-permute-start.4
  17.9 0.0 collective-permute-done.3.refs_4_.refs_9_
  17.9 0.5 collective-permute-start.5
  18.4 0.0 collective-permute-done.7.refs_5_
  18.4 0.1 collective-permute-start.6
  18.5 2.7 %collective-permute-done.8.refs_6_ = bf16[8,3072]{1,0:T(8,128)(2,1)S(1)} collective-permute-done((bf16[8,3072]{1,0:T(8,128)(2,1)S(1)}, bf16[8,3072]{1,0:T(8,128)(2,1)S(1)}, u32[]{:S(2)}, u32[]{:S(2)}) %collective-permute-start.8) | collective-permute-done | bytes 49184 | tf_op jit(solution)/shard_map/ppermute | solution.py:240
  21.2 0.0 collective-permute-start.10
  21.2 2.5 %collective-permute-done.9.refs_7_ = bf16[8,3072]{1,0:T(8,128)(2,1)S(1)} collective-permute-done((bf16[8,3072]{1,0:T(8,128)(2,1)S(1)}, bf16[8,3072]{1,0:T(8,128)(2,1)S(1)}, u32[]{:S(2)}, u32[]{:S(2)}) %collective-permute-start.9) | collective-permute-done | bytes 49184 | tf_op jit(solution)/shard_map/ppermute | solution.py:240
  23.7 0.5 collective-permute-start.12
  24.2 0.1 collective-permute-start.13
  24.3 0.7 copy-done.8
  25.0 13.0 %shard_map.122 = (bf16[64,2304]{1,0:T(8,128)(2,1)S(1)}, f32[2304,64]{1,0:T(8,128)S(1)}, f32[2304,64]{1,0:T(8,128)S(1)}, f32[64,128]{1,0:T(8,128)S(1)}, bf16[3072...) custom-call(s32[1]{0:T(128)} %bitcast.1.part_ref, bf16[8,3072]{1,0:T(8,128)(2,1)S(1)} %get-tuple-element.42.refs_0_.refs_5_, ...), custom_call_target="tpu_custom_call" | custom-call | flops 1811939328 | bytes 28311552 | tf_op jit(solution)/shard_map/pallas_call | solution.py:29
  38.0 5.0 %copy-done = bf16[3072,2304]{1,0:T(8,128)(2,1)} copy-done((bf16[3072,2304]{1,0:T(8,128)(2,1)}, bf16[3072,2304]{1,0:T(8,128)(2,1)S(1)}, u32[]{:S(2)}) %copy-start) | copy-done | bytes 14155800
  43.1 0.0 copy-start.6
  43.1 12.0 %shard_map.123 = (f32[32,3072]{1,0:T(8,128)S(1)}, bf16[32,3072]{1,0:T(8,128)(2,1)S(1)}, bf16[2304,64]{1,0:T(8,128)(2,1)S(1)}, bf16[2304,64]{1,0:T(8,128)(2,1)S(1)}) custom-call(s32[1]{0:T(128)} %bitcast.1.part_ref, bf16[64,2304]{1,0:T(8,128)(2,1)S(1)} %get-tuple-element.46.refs_0_, f32[2304,64]{1,0:T(8,128)S(1)} %get-tuple-element.47.refs_1_, ...), custom_call_target="tpu_custom_call" | custom-call | flops 1811939328 | bytes 14155776 | tf_op jit(solution)/shard_map/pallas_call | solution.py:29
  55.1 0.5 collective-permute-start.14
  55.6 1.1 %collective-permute-done.14.other_ref = bf16[32,3072]{1,0:T(8,128)(2,1)S(1)} collective-permute-done((bf16[32,3072]{1,0:T(8,128)(2,1)S(1)}, bf16[32,3072]{1,0:T(8,128)(2,1)S(1)}, u32[]{:S(2)}, u32[]{:S(2)}) %collective-permute-start.14) | collective-permute-done | bytes 196640 | tf_op jit(solution)/shard_map/ppermute | solution.py:223
  56.7 0.1 collective-permute-start.15
  56.8 2.2 %collective-permute-start.16 = (bf16[8,3072]{1,0:T(8,128)(2,1)S(1)}, bf16[8,3072]{1,0:T(8,128)(2,1)S(1)}, u32[]{:S(2)}, u32[]{:S(2)}) collective-permute-start(bf16[8,3072]{1,0:T(8,128)(2,1)S(1)} %get-tuple-element.57), channel_id=1, source_target_pairs={{0,4},{2,6},{4,0},{6,2},{1,5},{3,7},{5,1},{7,3},{8,12},{10,14},{12... | collective-permute-start | bytes 147464 | tf_op jit(solution)/shard_map/ppermute | solution.py:240
  59.0 2.2 %collective-permute-start.17 = (bf16[8,3072]{1,0:T(8,128)(2,1)S(1)}, bf16[8,3072]{1,0:T(8,128)(2,1)S(1)}, u32[]{:S(2)}, u32[]{:S(2)}) collective-permute-start(bf16[8,3072]{1,0:T(8,128)(2,1)S(1)} %get-tuple-element.58), channel_id=1, source_target_pairs={{0,6},{2,4},{4,2},{6,0},{1,7},{3,5},{5,3},{7,1},{8,14},{10,12},{12... | collective-permute-start | bytes 147464 | tf_op jit(solution)/shard_map/ppermute | solution.py:240
  61.2 0.6 collective-permute-done.15.refs_1_
  61.7 0.9 collective-permute-done.16.refs_2_
  62.6 2.3 %collective-permute-done.17.refs_3_ = bf16[8,3072]{1,0:T(8,128)(2,1)S(1)} collective-permute-done((bf16[8,3072]{1,0:T(8,128)(2,1)S(1)}, bf16[8,3072]{1,0:T(8,128)(2,1)S(1)}, u32[]{:S(2)}, u32[]{:S(2)}) %collective-permute-start.17) | collective-permute-done | bytes 49184 | tf_op jit(solution)/shard_map/ppermute | solution.py:240
  64.9 0.4 shard_map.125
  65.3 1.6 %collective-permute-start.19 = (f32[16,128]{1,0:T(8,128)S(1)}, f32[16,128]{1,0:T(8,128)S(1)}, u32[]{:S(2)}, u32[]{:S(2)}) collective-permute-start(f32[16,128]{1,0:T(8,128)S(1)} %get-tuple-element.60.score_ref), channel_id=1, source_target_pairs={{0,1},{1,0},{2,3},{3,2},{4,5},{5,4},{6,7},{7,6},{8,9},{9,8},{10,11... | collective-permute-start | bytes 24584 | tf_op jit(solution)/shard_map/ppermute | solution.py:223
  66.9 0.5 collective-permute-start.18
  67.4 5.0 %copy-done.1 = bf16[3072,2304]{1,0:T(8,128)(2,1)S(1)} copy-done((bf16[3072,2304]{1,0:T(8,128)(2,1)S(1)}, bf16[3072,2304]{1,0:T(8,128)(2,1)}, u32[]{:S(2)}) %copy-start.1) | copy-done | bytes 14155800
  72.4 7.7 %shard_map.127 = (f32[32,3072]{1,0:T(8,128)S(1)}, bf16[32,3072]{1,0:T(8,128)(2,1)S(1)}, f32[1,3072]{1,0:T(1,128)S(1)}) custom-call(bf16[2304,64]{1,0:T(8,128)(2,1)S(1)} %get-tuple-element.64.refs_0_, bf16[2304,64]{1,0:T(8,128)(2,1)S(1)} %get-tuple-element.65.refs_1_, bf16[3072,2304]{1,0:T(8,128)(2,1)S(1)} %get-tuple-element.66.refs_2_, ...), custom_call_target="tpu_custom_call" | custom-call | flops 1811939328 | bytes 28311552 | tf_op jit(solution)/shard_map/pallas_call | solution.py:29
  80.2 0.1 collective-permute-start.20
  80.3 1.1 %shard_map.126 = (bf16[16,3072]{1,0:T(8,128)(2,1)}, f32[16,3072]{1,0:T(8,128)S(1)}, f32[5,3072]{1,0:T(8,128)S(1)}) custom-call(s32[16,2]{1,0:T(8,128)S(1)} %copy.22.ids_ref, bf16[16,3072]{1,0:T(8,128)(2,1)S(1)} %copy-done.4, bf16[16,3072]{1,0:T(8,128)(2,1)S(1)} %get-tuple-element.59.mine_ref, bf16[16,3072]{1,0:T(8,128)(2,1)S(1)} %collective-permute-done.18.other_ref, ...), custom_call_target="tpu_custom_call" | custom-call | tf_op jit(solution)/shard_map/pallas_call | solution.py:29
  81.4 0.8 all_to_all.13
  82.2 4.4 %all-to-all-start = ((f32[32,1,480]{2,1,0:T(1,128)}), f32[32,1,480]{2,1,0:T(1,128)S(1)}, u32[]{:S(2)}, u32[]{:S(2)}) async-start(f32[32,1,480]{2,1,0:T(1,128)} %all_to_all.13), calls=%async_computation | async-start | bytes 131072 | tf_op jit(solution)/shard_map/all_to_all | solution.py:268
  86.6 0.1 shard_map.128
  86.7 1.8 %collective-permute-start.21 = (bf16[8,3072]{1,0:T(8,128)(2,1)S(1)}, bf16[8,3072]{1,0:T(8,128)(2,1)S(1)}, u32[]{:S(2)}, u32[]{:S(2)}) collective-permute-start(bf16[8,3072]{1,0:T(8,128)(2,1)S(1)} %get-tuple-element.72), channel_id=1, source_target_pairs={{0,2},{2,0},{4,6},{6,4},{1,3},{3,1},{5,7},{7,5},{8,10},{10,8},{12,... | collective-permute-start | bytes 147464 | tf_op jit(solution)/shard_map/ppermute | solution.py:240
  88.5 2.4 %collective-permute-start.22 = (bf16[8,3072]{1,0:T(8,128)(2,1)S(1)}, bf16[8,3072]{1,0:T(8,128)(2,1)S(1)}, u32[]{:S(2)}, u32[]{:S(2)}) collective-permute-start(bf16[8,3072]{1,0:T(8,128)(2,1)S(1)} %get-tuple-element.73), channel_id=1, source_target_pairs={{0,4},{2,6},{4,0},{6,2},{1,5},{3,7},{5,1},{7,3},{8,12},{10,14},{12... | collective-permute-start | bytes 147464 | tf_op jit(solution)/shard_map/ppermute | solution.py:240
  91.0 0.2 collective-permute-start.23
  91.2 2.9 %all-to-all-done = f32[32,1,480]{2,1,0:T(1,128)S(1)} async-done(((f32[32,1,480]{2,1,0:T(1,128)}), f32[32,1,480]{2,1,0:T(1,128)S(1)}, u32[]{:S(2)}, u32[]{:S(2)}) %all-to-all-start) | async-done | bytes 61472 | tf_op jit(solution)/shard_map/all_to_all | solution.py:268
  94.1 0.1 reduce_sum.9
  94.2 0.7 broadcast_in_dim.2
  94.8 2.9 %all-to-all-start.1 = ((f32[32,1,480]{2,1,0:T(1,128)}), f32[32,1,480]{2,1,0:T(1,128)S(1)}, u32[]{:S(2)}, u32[]{:S(2)}) async-start(f32[32,1,480]{2,1,0:T(1,128)} %broadcast_in_dim.2), calls=%async_computation.1 | async-start | bytes 131072 | tf_op jit(solution)/shard_map/all_to_all | solution.py:271
  97.8 0.2 shard_map.129.mine_ref
  98.0 1.8 %collective-permute-start.24 = (bf16[16,3072]{1,0:T(8,128)(2,1)S(1)}, bf16[16,3072]{1,0:T(8,128)(2,1)S(1)}, u32[]{:S(2)}, u32[]{:S(2)}) collective-permute-start(bf16[16,3072]{1,0:T(8,128)(2,1)S(1)} %shard_map.129.mine_ref), channel_id=1, source_target_pairs={{0,1},{1,0},{2,3},{3,2},{4,5},{5,4},{6,7},{7,6},{8,9},{9,8},{10,11... | collective-permute-start | bytes 294920 | tf_op jit(solution)/shard_map/ppermute | solution.py:223
  99.8 3.6 %collective-permute-done.24.other_ref = bf16[16,3072]{1,0:T(8,128)(2,1)S(1)} collective-permute-done((bf16[16,3072]{1,0:T(8,128)(2,1)S(1)}, bf16[16,3072]{1,0:T(8,128)(2,1)S(1)}, u32[]{:S(2)}, u32[]{:S(2)}) %collective-permute-start.24) | collective-permute-done | bytes 98336 | tf_op jit(solution)/shard_map/ppermute | solution.py:223
  103.5 0.8 shard_map.130
  104.3 0.7 all-to-all-done.1
  105.0 0.2 reduce.1
  105.2 0.1 reshape.30
  105.3 0.6 slice.17
  105.9 0.6 slice_bitcast_fusion
  (37 shorter events, 0.2 us)
Async XLA Ops:
  2.2 0.9 copy-start.2
  3.3 11.0 %collective-permute-start = (bf16[8,3072]{1,0:T(8,128)(2,1)S(1)}, bf16[8,3072]{1,0:T(8,128)(2,1)S(1)}, u32[]{:S(2)}, u32[]{:S(2)}) collective-permute-start(bf16[8,3072]{1,0:T(8,128)(2,1)S(1)} %get-tuple-element.43), channel_id=1, source_target_pairs={{0,2},{2,0},{4,6},{6,4},{1,3},{3,1},{5,7},{7,5},{8,10},{10,8},{12,... | collective-permute-start | bytes 147464 | tf_op jit(solution)/shard_map/ppermute | solution.py:240
  6.5 11.4 %collective-permute-start.1 = (bf16[8,3072]{1,0:T(8,128)(2,1)S(1)}, bf16[8,3072]{1,0:T(8,128)(2,1)S(1)}, u32[]{:S(2)}, u32[]{:S(2)}) collective-permute-start(bf16[8,3072]{1,0:T(8,128)(2,1)S(1)} %get-tuple-element.44), channel_id=1, source_target_pairs={{0,4},{2,6},{4,0},{6,2},{1,5},{3,7},{5,1},{7,3},{8,12},{10,14},{12... | collective-permute-start | bytes 147464 | tf_op jit(solution)/shard_map/ppermute | solution.py:240
  9.1 8.8 %collective-permute-start.2 = (bf16[8,3072]{1,0:T(8,128)(2,1)S(1)}, bf16[8,3072]{1,0:T(8,128)(2,1)S(1)}, u32[]{:S(2)}, u32[]{:S(2)}) collective-permute-start(bf16[8,3072]{1,0:T(8,128)(2,1)S(1)} %get-tuple-element.45), channel_id=1, source_target_pairs={{0,6},{2,4},{4,2},{6,0},{1,7},{3,5},{5,3},{7,1},{8,14},{10,12},{12... | collective-permute-start | bytes 147464 | tf_op jit(solution)/shard_map/ppermute | solution.py:240
  9.1 8.8 %collective-permute-start.3 = (bf16[8,3072]{1,0:T(8,128)(2,1)S(1)}, bf16[8,3072]{1,0:T(8,128)(2,1)S(1)}, u32[]{:S(2)}, u32[]{:S(2)}) collective-permute-start(bf16[8,3072]{1,0:T(8,128)(2,1)S(1)} %get-tuple-element.42.refs_0_.refs_5_), channel_id=1, source_target_pairs={{0,8},{8,0},{16,24},{24,16},{1,9},{9,1},{17,25},{25,17},{2,10},{10... | collective-permute-start | bytes 147464 | tf_op jit(solution)/shard_map/ppermute | solution.py:223
  10.2 0.9 copy-start.3
  11.1 0.9 copy-start.5
  12.0 0.7 copy-start.7
  13.4 5.0 %collective-permute-start.7 = (bf16[8,3072]{1,0:T(8,128)(2,1)S(1)}, bf16[8,3072]{1,0:T(8,128)(2,1)S(1)}, u32[]{:S(2)}, u32[]{:S(2)}) collective-permute-start(bf16[8,3072]{1,0:T(8,128)(2,1)S(1)} %get-tuple-element.50), channel_id=1, source_target_pairs={{0,2},{2,0},{4,6},{6,4},{1,3},{3,1},{5,7},{7,5},{8,10},{10,8},{12,... | collective-permute-start | bytes 147464 | tf_op jit(solution)/shard_map/ppermute | solution.py:240
  14.3 6.9 %collective-permute-start.8 = (bf16[8,3072]{1,0:T(8,128)(2,1)S(1)}, bf16[8,3072]{1,0:T(8,128)(2,1)S(1)}, u32[]{:S(2)}, u32[]{:S(2)}) collective-permute-start(bf16[8,3072]{1,0:T(8,128)(2,1)S(1)} %get-tuple-element.51), channel_id=1, source_target_pairs={{0,4},{2,6},{4,0},{6,2},{1,5},{3,7},{5,1},{7,3},{8,12},{10,14},{12... | collective-permute-start | bytes 147464 | tf_op jit(solution)/shard_map/ppermute | solution.py:240
  17.8 5.9 %collective-permute-start.9 = (bf16[8,3072]{1,0:T(8,128)(2,1)S(1)}, bf16[8,3072]{1,0:T(8,128)(2,1)S(1)}, u32[]{:S(2)}, u32[]{:S(2)}) collective-permute-start(bf16[8,3072]{1,0:T(8,128)(2,1)S(1)} %get-tuple-element.52), channel_id=1, source_target_pairs={{0,6},{2,4},{4,2},{6,0},{1,7},{3,5},{5,3},{7,1},{8,14},{10,12},{12... | collective-permute-start | bytes 147464 | tf_op jit(solution)/shard_map/ppermute | solution.py:240
  17.8 5.9 %collective-permute-start.4 = (bf16[8,3072]{1,0:T(8,128)(2,1)S(1)}, bf16[8,3072]{1,0:T(8,128)(2,1)S(1)}, u32[]{:S(2)}, u32[]{:S(2)}) collective-permute-start(bf16[8,3072]{1,0:T(8,128)(2,1)S(1)} %collective-permute-done.refs_1_.refs_6_), channel_id=1, source_target_pairs={{0,8},{8,0},{16,24},{24,16},{1,9},{9,1},{17,25},{25,17},{2,10},{10... | collective-permute-start | bytes 147464 | tf_op jit(solution)/shard_map/ppermute | solution.py:223
  17.9 6.3 %collective-permute-start.5 = (bf16[8,3072]{1,0:T(8,128)(2,1)S(1)}, bf16[8,3072]{1,0:T(8,128)(2,1)S(1)}, u32[]{:S(2)}, u32[]{:S(2)}) collective-permute-start(bf16[8,3072]{1,0:T(8,128)(2,1)S(1)} %collective-permute-done.1.refs_2_.refs_7_), channel_id=1, source_target_pairs={{0,8},{8,0},{16,24},{24,16},{1,9},{9,1},{17,25},{25,17},{2,10},{10... | collective-permute-start | bytes 147464 | tf_op jit(solution)/shard_map/ppermute | solution.py:223
  18.4 5.9 %collective-permute-start.6 = (bf16[8,3072]{1,0:T(8,128)(2,1)S(1)}, bf16[8,3072]{1,0:T(8,128)(2,1)S(1)}, u32[]{:S(2)}, u32[]{:S(2)}) collective-permute-start(bf16[8,3072]{1,0:T(8,128)(2,1)S(1)} %collective-permute-done.2.refs_3_.refs_8_), channel_id=1, source_target_pairs={{0,8},{8,0},{16,24},{24,16},{1,9},{9,1},{17,25},{25,17},{2,10},{10... | collective-permute-start | bytes 147464 | tf_op jit(solution)/shard_map/ppermute | solution.py:223
  21.2 21.9 %collective-permute-start.10 = (bf16[8,3072]{1,0:T(8,128)(2,1)S(1)}, bf16[8,3072]{1,0:T(8,128)(2,1)S(1)}, u32[]{:S(2)}, u32[]{:S(2)}) collective-permute-start(bf16[8,3072]{1,0:T(8,128)(2,1)S(1)} %get-tuple-element.49.refs_4_), channel_id=1, source_target_pairs={{0,8},{8,0},{16,24},{24,16},{1,9},{9,1},{17,25},{25,17},{2,10},{10... | collective-permute-start | bytes 147464 | tf_op jit(solution)/shard_map/ppermute | solution.py:223
  23.7 19.4 %collective-permute-start.11 = (bf16[8,3072]{1,0:T(8,128)(2,1)S(1)}, bf16[8,3072]{1,0:T(8,128)(2,1)S(1)}, u32[]{:S(2)}, u32[]{:S(2)}) collective-permute-start(bf16[8,3072]{1,0:T(8,128)(2,1)S(1)} %collective-permute-done.7.refs_5_), channel_id=1, source_target_pairs={{0,8},{8,0},{16,24},{24,16},{1,9},{9,1},{17,25},{25,17},{2,10},{10... | collective-permute-start | bytes 147464 | tf_op jit(solution)/shard_map/ppermute | solution.py:223
  23.7 19.4 %collective-permute-start.12 = (bf16[8,3072]{1,0:T(8,128)(2,1)S(1)}, bf16[8,3072]{1,0:T(8,128)(2,1)S(1)}, u32[]{:S(2)}, u32[]{:S(2)}) collective-permute-start(bf16[8,3072]{1,0:T(8,128)(2,1)S(1)} %collective-permute-done.8.refs_6_), channel_id=1, source_target_pairs={{0,8},{8,0},{16,24},{24,16},{1,9},{9,1},{17,25},{25,17},{2,10},{10... | collective-permute-start | bytes 147464 | tf_op jit(solution)/shard_map/ppermute | solution.py:223
  24.2 18.9 %collective-permute-start.13 = (bf16[8,3072]{1,0:T(8,128)(2,1)S(1)}, bf16[8,3072]{1,0:T(8,128)(2,1)S(1)}, u32[]{:S(2)}, u32[]{:S(2)}) collective-permute-start(bf16[8,3072]{1,0:T(8,128)(2,1)S(1)} %collective-permute-done.9.refs_7_), channel_id=1, source_target_pairs={{0,8},{8,0},{16,24},{24,16},{1,9},{9,1},{17,25},{25,17},{2,10},{10... | collective-permute-start | bytes 147464 | tf_op jit(solution)/shard_map/ppermute | solution.py:223
  24.3 0.7 copy-start.8
  38.0 5.0 %copy-start = (bf16[3072,2304]{1,0:T(8,128)(2,1)}, bf16[3072,2304]{1,0:T(8,128)(2,1)S(1)}, u32[]{:S(2)}) copy-start(bf16[3072,2304]{1,0:T(8,128)(2,1)S(1)} %get-tuple-element.67.refs_3_) | copy-start | bytes 42467332
  43.1 21.9 %copy-start.6 = (bf16[16,3072]{1,0:T(8,128)(2,1)S(1)}, bf16[16,3072]{1,0:T(8,128)(2,1)}, u32[]{:S(2)}) copy-start(bf16[16,3072]{1,0:T(8,128)(2,1)} %cotangent_ref.5) | copy-start | bytes 294916
  55.1 1.6 %collective-permute-start.14 = (bf16[32,3072]{1,0:T(8,128)(2,1)S(1)}, bf16[32,3072]{1,0:T(8,128)(2,1)S(1)}, u32[]{:S(2)}, u32[]{:S(2)}) collective-permute-start(bf16[32,3072]{1,0:T(8,128)(2,1)S(1)} %get-tuple-element.54), channel_id=1, source_target_pairs={{0,8},{8,0},{16,24},{24,16},{1,9},{9,1},{17,25},{25,17},{2,10},{10... | collective-permute-start | bytes 589832 | tf_op jit(solution)/shard_map/ppermute | solution.py:223
  56.7 5.0 %collective-permute-start.15 = (bf16[8,3072]{1,0:T(8,128)(2,1)S(1)}, bf16[8,3072]{1,0:T(8,128)(2,1)S(1)}, u32[]{:S(2)}, u32[]{:S(2)}) collective-permute-start(bf16[8,3072]{1,0:T(8,128)(2,1)S(1)} %get-tuple-element.56), channel_id=1, source_target_pairs={{0,2},{2,0},{4,6},{6,4},{1,3},{3,1},{5,7},{7,5},{8,10},{10,8},{12,... | collective-permute-start | bytes 147464 | tf_op jit(solution)/shard_map/ppermute | solution.py:240
  56.8 5.8 %collective-permute-start.16 = (bf16[8,3072]{1,0:T(8,128)(2,1)S(1)}, bf16[8,3072]{1,0:T(8,128)(2,1)S(1)}, u32[]{:S(2)}, u32[]{:S(2)}) collective-permute-start(bf16[8,3072]{1,0:T(8,128)(2,1)S(1)} %get-tuple-element.57), channel_id=1, source_target_pairs={{0,4},{2,6},{4,0},{6,2},{1,5},{3,7},{5,1},{7,3},{8,12},{10,14},{12... | collective-permute-start | bytes 147464 | tf_op jit(solution)/shard_map/ppermute | solution.py:240
  59.0 6.0 %collective-permute-start.17 = (bf16[8,3072]{1,0:T(8,128)(2,1)S(1)}, bf16[8,3072]{1,0:T(8,128)(2,1)S(1)}, u32[]{:S(2)}, u32[]{:S(2)}) collective-permute-start(bf16[8,3072]{1,0:T(8,128)(2,1)S(1)} %get-tuple-element.58), channel_id=1, source_target_pairs={{0,6},{2,4},{4,2},{6,0},{1,7},{3,5},{5,3},{7,1},{8,14},{10,12},{12... | collective-permute-start | bytes 147464 | tf_op jit(solution)/shard_map/ppermute | solution.py:240
  65.3 14.9 %collective-permute-start.19 = (f32[16,128]{1,0:T(8,128)S(1)}, f32[16,128]{1,0:T(8,128)S(1)}, u32[]{:S(2)}, u32[]{:S(2)}) collective-permute-start(f32[16,128]{1,0:T(8,128)S(1)} %get-tuple-element.60.score_ref), channel_id=1, source_target_pairs={{0,1},{1,0},{2,3},{3,2},{4,5},{5,4},{6,7},{7,6},{8,9},{9,8},{10,11... | collective-permute-start | bytes 24584 | tf_op jit(solution)/shard_map/ppermute | solution.py:223
  66.9 13.4 %collective-permute-start.18 = (bf16[16,3072]{1,0:T(8,128)(2,1)S(1)}, bf16[16,3072]{1,0:T(8,128)(2,1)S(1)}, u32[]{:S(2)}, u32[]{:S(2)}) collective-permute-start(bf16[16,3072]{1,0:T(8,128)(2,1)S(1)} %get-tuple-element.59.mine_ref), channel_id=1, source_target_pairs={{0,1},{1,0},{2,3},{3,2},{4,5},{5,4},{6,7},{7,6},{8,9},{9,8},{10,11... | collective-permute-start | bytes 294920 | tf_op jit(solution)/shard_map/ppermute | solution.py:223
  67.4 5.0 %copy-start.1 = (bf16[3072,2304]{1,0:T(8,128)(2,1)S(1)}, bf16[3072,2304]{1,0:T(8,128)(2,1)}, u32[]{:S(2)}) copy-start(bf16[3072,2304]{1,0:T(8,128)(2,1)} %copy-done) | copy-start | bytes 42467332
  72.4 7.8 %copy-start.4 = (bf16[16,3072]{1,0:T(8,128)(2,1)S(1)}, bf16[16,3072]{1,0:T(8,128)(2,1)}, u32[]{:S(2)}) copy-start(bf16[16,3072]{1,0:T(8,128)(2,1)} %tokens_ref.7) | copy-start | bytes 294916
  72.4 7.9 %copy-start.10 = (bf16[3072,4]{0,1:T(4,128)(2,1)S(1)}, bf16[3072,4]{0,1:T(4,128)(2,1)}, u32[]{:S(2)}) copy-start(bf16[3072,4]{0,1:T(4,128)(2,1)} %param.12) | copy-start | bytes 73732
  72.4 31.0 %copy-start.9 = (f32[3072]{0:T(1024)S(1)}, f32[3072]{0:T(1024)}, u32[]{:S(2)}) copy-start(f32[3072]{0:T(1024)} %param.11) | copy-start | bytes 36868
  80.2 6.5 %collective-permute-start.20 = (bf16[32,3072]{1,0:T(8,128)(2,1)S(1)}, bf16[32,3072]{1,0:T(8,128)(2,1)S(1)}, u32[]{:S(2)}, u32[]{:S(2)}) collective-permute-start(bf16[32,3072]{1,0:T(8,128)(2,1)S(1)} %get-tuple-element.70), channel_id=1, source_target_pairs={{0,8},{8,0},{16,24},{24,16},{1,9},{9,1},{17,25},{25,17},{2,10},{10... | collective-permute-start | bytes 589832 | tf_op jit(solution)/shard_map/ppermute | solution.py:223
  82.2 11.9 %all-to-all-start = ((f32[32,1,480]{2,1,0:T(1,128)}), f32[32,1,480]{2,1,0:T(1,128)S(1)}, u32[]{:S(2)}, u32[]{:S(2)}) async-start(f32[32,1,480]{2,1,0:T(1,128)} %all_to_all.13), calls=%async_computation | async-start | bytes 131072 | tf_op jit(solution)/shard_map/all_to_all | solution.py:268
  86.7 11.0 %collective-permute-start.21 = (bf16[8,3072]{1,0:T(8,128)(2,1)S(1)}, bf16[8,3072]{1,0:T(8,128)(2,1)S(1)}, u32[]{:S(2)}, u32[]{:S(2)}) collective-permute-start(bf16[8,3072]{1,0:T(8,128)(2,1)S(1)} %get-tuple-element.72), channel_id=1, source_target_pairs={{0,2},{2,0},{4,6},{6,4},{1,3},{3,1},{5,7},{7,5},{8,10},{10,8},{12,... | collective-permute-start | bytes 147464 | tf_op jit(solution)/shard_map/ppermute | solution.py:240
  88.5 9.2 %collective-permute-start.22 = (bf16[8,3072]{1,0:T(8,128)(2,1)S(1)}, bf16[8,3072]{1,0:T(8,128)(2,1)S(1)}, u32[]{:S(2)}, u32[]{:S(2)}) collective-permute-start(bf16[8,3072]{1,0:T(8,128)(2,1)S(1)} %get-tuple-element.73), channel_id=1, source_target_pairs={{0,4},{2,6},{4,0},{6,2},{1,5},{3,7},{5,1},{7,3},{8,12},{10,14},{12... | collective-permute-start | bytes 147464 | tf_op jit(solution)/shard_map/ppermute | solution.py:240
  91.0 6.8 %collective-permute-start.23 = (bf16[8,3072]{1,0:T(8,128)(2,1)S(1)}, bf16[8,3072]{1,0:T(8,128)(2,1)S(1)}, u32[]{:S(2)}, u32[]{:S(2)}) collective-permute-start(bf16[8,3072]{1,0:T(8,128)(2,1)S(1)} %get-tuple-element.74), channel_id=1, source_target_pairs={{0,6},{2,4},{4,2},{6,0},{1,7},{3,5},{5,3},{7,1},{8,14},{10,12},{12... | collective-permute-start | bytes 147464 | tf_op jit(solution)/shard_map/ppermute | solution.py:240
  94.8 10.2 %all-to-all-start.1 = ((f32[32,1,480]{2,1,0:T(1,128)}), f32[32,1,480]{2,1,0:T(1,128)S(1)}, u32[]{:S(2)}, u32[]{:S(2)}) async-start(f32[32,1,480]{2,1,0:T(1,128)} %broadcast_in_dim.2), calls=%async_computation.1 | async-start | bytes 131072 | tf_op jit(solution)/shard_map/all_to_all | solution.py:271
  98.0 5.5 %collective-permute-start.24 = (bf16[16,3072]{1,0:T(8,128)(2,1)S(1)}, bf16[16,3072]{1,0:T(8,128)(2,1)S(1)}, u32[]{:S(2)}, u32[]{:S(2)}) collective-permute-start(bf16[16,3072]{1,0:T(8,128)(2,1)S(1)} %shard_map.129.mine_ref), channel_id=1, source_target_pairs={{0,1},{1,0},{2,3},{3,2},{4,5},{5,4},{6,7},{7,6},{8,9},{9,8},{10,11... | collective-permute-start | bytes 294920 | tf_op jit(solution)/shard_map/ppermute | solution.py:223

commit v2 on v1

v2 whole, which is shorter than its diff:
```python
import functools

import jax
import jax.numpy as jnp
from jax import lax
from jax.experimental import pallas as pl
from jax.experimental.pallas import tpu as pltpu
from jax.sharding import PartitionSpec as P


epsilon = 1e-05
MIB = 1 << 20
VMEM = pl.BlockSpec(memory_space=pltpu.VMEM)
SMEM = pl.BlockSpec(memory_space=pltpu.SMEM)
HBM = pl.BlockSpec(memory_space=pltpu.HBM)
NN = (((1,), (0,)), ((), ()))
NT = (((1,), (1,)), ((), ()))
TN = (((0,), (0,)), ((), ()))


def mm(a, b, dims):
    return lax.dot_general(a, b, dims, preferred_element_type=jnp.float32)


def shape(dims, dtype):
    return jax.ShapeDtypeStruct(dims, dtype)


def call(body, ins, in_specs, outs, scratch=(), limit=3, flops=0, moved=0):
    return pl.pallas_call(
        body,
        in_specs=in_specs,
        out_specs=[VMEM] * len(outs),
        out_shape=outs,
        scratch_shapes=scratch,
        compiler_params=pltpu.CompilerParams(vmem_limit_bytes=limit * MIB),
        cost_estimate=pl.CostEstimate(flops=flops, bytes_accessed=moved, transcendentals=0),
    )(*ins)


def piece(size):
    for width in (256, 128):
        if size % width == 0:
            return width
    return size


def load_all(pairs, sems):
    copies = [pltpu.make_async_copy(src, dst, sems.at[i]) for i, (src, dst) in enumerate(pairs)]
    for copy in copies:
        copy.start()
    for copy in copies:
        copy.wait()


def column(row):
    size = row.shape[1]
    across = lax.broadcasted_iota(jnp.int32, (size, size), 0)
    along = lax.broadcasted_iota(jnp.int32, (size, size), 1)
    return jnp.sum(jnp.where(across == along, row, 0.0), axis=1, keepdims=True)


def prepare(experts, capacity, paired, places_ref, ids_any, slots_any, tokens_any, cotangent_any, gain_any, router_any, *refs):
    outs = refs[: experts if paired else 2]
    first_ref, second_ref, probs_ref, inv_ref, signs_ref, normed_ref = refs[len(outs) : len(outs) + 6]
    tokens_ref, cotangent_ref, gain_ref, router_ref, ids_ref, slots_ref, sems = refs[len(outs) + 6 :]
    load_all(
        (
            (ids_any, ids_ref),
            (slots_any, slots_ref),
            (tokens_any, tokens_ref),
            (cotangent_any, cotangent_ref),
            (gain_any, gain_ref),
            (router_any, router_ref),
        ),
        sems,
    )
    rows = experts * capacity
    ids = ids_ref[...]
    owner = (ids ^ places_ref[0]) if paired else ids
    index = owner * capacity + slots_ref[...]
    places = lax.broadcasted_iota(jnp.int32, (rows, index.shape[1]), 0)
    first = places == index[0:1, :]
    second = places == index[1:2, :]
    first_ref[...] = first.astype(jnp.bfloat16)
    second_ref[...] = second.astype(jnp.bfloat16)
    select = (first | second).astype(jnp.bfloat16)
    tokens = tokens_ref[...]
    inputs = mm(select, tokens, NN)
    floats = tokens.astype(jnp.float32)
    inv = lax.rsqrt(jnp.mean(floats * floats, axis=1, keepdims=True) + epsilon)
    normed = (floats * inv * gain_ref[...]).astype(jnp.bfloat16)
    logits = mm(router_ref[...], normed, NT)
    names = lax.broadcasted_iota(jnp.int32, (experts, ids.shape[1]), 0)
    signs = (names == ids[0:1, :]).astype(jnp.float32) - (names == ids[1:2, :]).astype(jnp.float32)
    prob = jax.nn.sigmoid(jnp.sum(signs * logits, axis=0, keepdims=True))
    weights = jnp.sum(jnp.where(first, prob, 0.0) + jnp.where(second, 1.0 - prob, 0.0), axis=1, keepdims=True)
    grads = weights * mm(select, cotangent_ref[...], NN)
    if paired:
        for expert, ref in enumerate(outs):
            mine = slice(expert * capacity, (expert + 1) * capacity)
            ref[...] = jnp.concatenate([inputs[mine], grads[mine]], axis=0).astype(jnp.bfloat16)
    else:
        outs[0][...] = inputs.astype(jnp.bfloat16)
        outs[1][...] = grads.astype(jnp.bfloat16)
    probs_ref[...] = jnp.broadcast_to(column(prob), probs_ref.shape)
    inv_ref[...] = jnp.broadcast_to(inv, inv_ref.shape)
    normed_ref[...] = normed
    for expert in range(experts):
        signs_ref[:, expert : expert + 1] = column(signs[expert : expert + 1, :])


def fetch(places_ref, gate_ref, gate_out, sems):
    width = gate_out.shape[1]
    columns = pl.ds(pl.multiple_of(places_ref[1] * width, width), width)
    load_all(((gate_ref.at[:, columns], gate_out),), sems)


def stack(refs, paired=False, half=0):
    values = []
    for ref in refs:
        value = ref[...].astype(jnp.float32)
        if paired:
            rows = value.shape[0] // 2
            value = value[half * rows : (half + 1) * rows]
        values.append(value)
    return jnp.concatenate(values, axis=0)


def split(value, refs):
    rows = refs[0].shape[0]
    for place, ref in enumerate(refs):
        ref[...] = value[place * rows : (place + 1) * rows].astype(ref.dtype)


MIDDLE_FLIGHT = 3


def forward(count, paired, places_ref, *refs):
    tokens_refs = refs[:count]
    gain_ref, gate_ref, up_any, act_ref, slope_ref, silu_ref, scaled_ref, up_ref, sems = refs[count:]
    inner = act_ref.shape[1]
    width = piece(inner)
    copies = []
    for step in range(inner // width):
        there = pl.ds(pl.multiple_of(places_ref[1] * inner + step * width, width), width)
        here = up_ref.at[:, pl.ds(step * width, width)]
        copies.append(pltpu.make_async_copy(up_any.at[:, there], here, sems.at[step]))
        copies[step].start()
    floats = stack(tokens_refs, paired, 0)
    inv = lax.rsqrt(jnp.mean(floats * floats, axis=1, keepdims=True) + epsilon)
    scaled = floats * inv
    scaled_ref[...] = scaled
    normed = (scaled * gain_ref[...]).astype(jnp.bfloat16)
    for step in range(inner // width):
        span = pl.ds(step * width, width)
        gate = mm(normed, gate_ref[:, span], NN)
        copies[step].wait()
        up = mm(normed, up_ref[:, span], NN)
        sigmoid = jax.nn.sigmoid(gate)
        silu = gate * sigmoid
        act_ref[:, span] = (silu * up).astype(jnp.bfloat16)
        slope_ref[span, :] = (up * sigmoid * (1.0 + gate * (1.0 - sigmoid))).T
        silu_ref[span, :] = silu.T


def middle(count, paired, places_ref, act_ref, slope_ref, silu_ref, down_any, *refs):
    *value_refs, gate_ref, up_ref, total_ref, down_ref, sems = refs[count:]
    slots, height, _ = down_ref.shape
    inner = act_ref.shape[1]
    steps = inner // height

    def copy(step):
        there = pl.ds(pl.multiple_of(places_ref[1] * inner + step * height, height), height)
        return pltpu.make_async_copy(down_any.at[there, :], down_ref.at[step % slots], sems.at[step % slots])

    ahead = min(slots, steps) - 1
    for step in range(ahead):
        copy(step).start()
    grads = stack(refs[:count], paired, 1).T.astype(jnp.bfloat16)
    for step in range(steps):
        span = pl.ds(step * height, height)
        copy(step).wait()
        if step + ahead < steps:
            copy(step + ahead).start()
        down = down_ref.at[step % slots]
        grad_act = mm(down[...], grads, NN)
        value = mm(act_ref[:, span], down[...], NN)
        total_ref[...] = value if step == 0 else total_ref[...] + value
        gate_ref[span, :] = (grad_act * slope_ref[span, :]).astype(jnp.bfloat16)
        up_ref[span, :] = (grad_act * silu_ref[span, :]).astype(jnp.bfloat16)
    split(total_ref[...], value_refs)


def backward(gate_grad_ref, up_grad_ref, gate_ref, up_ref, scaled_ref, *refs):
    *value_refs, gain_ref = refs
    rows = value_refs[0].shape[0]
    height = piece(gate_ref.shape[0])
    for start in range(0, gate_ref.shape[0], height):
        span = pl.ds(start, height)
        back = mm(gate_ref[span, :], gate_grad_ref[...], NN) + mm(up_ref[span, :], up_grad_ref[...], NN)
        back = back.T
        for part, value_ref in enumerate(value_refs):
            value_ref[:, span] = back[part * rows : (part + 1) * rows].astype(value_ref.dtype)
        gain_ref[:, span] = jnp.sum(back * scaled_ref[:, span], axis=0, keepdims=True)


def add_pair(own_ref, other_ref, *refs):
    split(own_ref[...] + other_ref[...].astype(jnp.float32), refs)


def round_own(own_ref, *refs):
    split(own_ref[...], refs)


def mix_values(first_ref, second_ref, probs_ref, inv_ref, signs_ref, normed_ref, tokens_ref, cotangent_ref, router_ref, gain_part_ref, *refs):
    *rows_refs, mix_ref, sums_ref = refs
    rows = stack(rows_refs).astype(jnp.bfloat16)
    first = mm(first_ref[...], rows, TN)
    second = mm(second_ref[...], rows, TN)
    width = first.shape[1]
    prob = probs_ref[:, :1]
    mix_ref[:, :width] = (prob * first + (1.0 - prob) * second).astype(jnp.bfloat16)
    score = jnp.sum(cotangent_ref[...].astype(jnp.float32) * (first - second), axis=1, keepdims=True)
    coarse = score.astype(jnp.bfloat16)
    fine = (score - coarse.astype(jnp.float32)).astype(jnp.bfloat16)
    mix_ref[:, width:] = jnp.zeros((mix_ref.shape[0], mix_ref.shape[1] - width), jnp.bfloat16)
    mix_ref[:, width : width + 1] = coarse
    mix_ref[:, width + 1 : width + 2] = fine
    grad_first = prob * (1.0 - prob) * score
    normed = normed_ref[...].astype(jnp.float32)
    term = jnp.zeros(first.shape, jnp.float32)
    experts = router_ref.shape[0]
    sums = []
    for expert in range(experts):
        column = grad_first * signs_ref[:, expert : expert + 1]
        term += column * router_ref[expert : expert + 1, :].astype(jnp.float32)
        sums.append(jnp.sum(column * normed, axis=0, keepdims=True))
    scaled = tokens_ref[...].astype(jnp.float32) * inv_ref[:, :1]
    sums.append(jnp.sum(term * scaled, axis=0, keepdims=True) + gain_part_ref[...])
    spread(sums, sums_ref)


def spread(rows, out_ref):
    lanes = 128
    across = out_ref.shape[1] // lanes
    place = 0
    for row in rows:
        for start in range(0, row.shape[1], lanes):
            top, left = place // across, place % across * lanes
            out_ref[top : top + 1, left : left + lanes] = row[:, start : start + lanes]
            place += 1
    while place < out_ref.shape[0] * across:
        top, left = place // across, place % across * lanes
        out_ref[top : top + 1, left : left + lanes] = jnp.zeros((1, lanes), jnp.float32)
        place += 1


def unpack(sums, router_ref, gain_ref):
    lanes = 128
    across = sums.shape[1] // lanes
    steps = gain_ref.shape[1] // lanes
    experts = router_ref.shape[0]
    for expert in range(experts + 1):
        out_ref, row = (router_ref, expert) if expert < experts else (gain_ref, 0)
        for step in range(steps):
            place = expert * steps + step
            top, left = place // across, place % across * lanes
            value = sums[top : top + 1, left : left + lanes]
            out_ref[row : row + 1, step * lanes : (step + 1) * lanes] = value


def gather_sums(sums_ref, router_ref, gain_ref):
    unpack(sums_ref, router_ref, gain_ref)


def add_all(own_ref, other_ref, sums_ref, other_sums_ref, *refs):
    rows = refs[0].shape[0]
    width = own_ref.shape[1]
    total = own_ref[...] + other_ref[...].astype(jnp.float32)
    sums = (sums_ref[...] + other_sums_ref[...]).astype(jnp.bfloat16)
    for place, ref in enumerate(refs):
        ref[:, :width] = total[place * rows : (place + 1) * rows].astype(jnp.bfloat16)
        ref[:, width:] = sums


def tree(values):
    while len(values) > 1:
        values = [a + b for a, b in zip(values[::2], values[1::2])]
    return values[0]


def mix_tokens(tokens_ref, mix_ref, other_mix_ref, mixed_ref):
    floats = tokens_ref[...].astype(jnp.float32)
    width = floats.shape[1]
    mine = mix_ref[...].astype(jnp.float32)
    other = other_mix_ref[...].astype(jnp.float32)
    mixed_ref[...] = (floats + (mine[:, :width] + other[:, :width])).astype(jnp.bfloat16)
    return (mine[:, width : width + 1] + mine[:, width + 1 : width + 2]) + (
        other[:, width : width + 1] + other[:, width + 1 : width + 2]
    )


def sum_all(first_ref, second_ref, tokens_ref, mix_ref, other_mix_ref, *refs):
    *rows_refs, out_ref, sums_ref, mixed_ref, score_ref = refs
    score_ref[...] = jnp.broadcast_to(mix_tokens(tokens_ref, mix_ref, other_mix_ref, mixed_ref), score_ref.shape)
    width = rows_refs[0].shape[1] - sums_ref.shape[1]
    rows = jnp.concatenate([ref[:, :width].astype(jnp.float32) for ref in rows_refs], axis=0).astype(jnp.bfloat16)
    out_ref[:, :width] = mm(first_ref[...] + second_ref[...], rows, TN).astype(jnp.bfloat16)
    sums = tree([ref[:, width:].astype(jnp.float32) for ref in rows_refs])
    sums_ref[...] = sums.astype(jnp.bfloat16)
    half = out_ref.shape[1] - width
    left, right = sums[:, :half], sums[:, half:]
    if right.shape[1] < half:
        right = jnp.concatenate([right, jnp.zeros((right.shape[0], half - right.shape[1]), jnp.float32)], axis=1)
    out_ref[:, width:] = jnp.concatenate([left, right], axis=0).astype(jnp.bfloat16)


def sum_rows(first_ref, second_ref, *refs):
    *rows_refs, out_ref = refs
    rows = stack(rows_refs).astype(jnp.bfloat16)
    out_ref[...] = mm(first_ref[...] + second_ref[...], rows, TN).astype(jnp.bfloat16)


def finish(joint, tokens_ref, cotangent_ref, gain_ref, router_ref, probs_ref, inv_ref, signs_ref, back_ref, other_back_ref, *refs):
    floats = tokens_ref[...].astype(jnp.float32)
    width = floats.shape[1]
    if joint:
        score_ref, sums_ref, side_ref, corner_ref, grads_ref, router_out, gain_out = refs
        score = score_ref[:, :1]
        rows, total = sums_ref.shape
        beside = other_back_ref[:, width:].astype(jnp.float32)
        beside = jnp.concatenate([beside[:rows], beside[rows:]], axis=1)[:, :total]
        mine = sums_ref[...].astype(jnp.float32) + beside
        unpack(mine + (side_ref[...].astype(jnp.float32) + corner_ref[...].astype(jnp.float32)), router_out, gain_out)
    else:
        mix_ref, other_mix_ref, mixed_ref, grads_ref = refs
        score = mix_tokens(tokens_ref, mix_ref, other_mix_ref, mixed_ref)
    prob = probs_ref[:, :1]
    inv = inv_ref[:, :1]
    grad_first = prob * (1.0 - prob) * score
    grad_normed = back_ref[:, :width].astype(jnp.float32) + other_back_ref[:, :width].astype(jnp.float32)
    for expert in range(router_ref.shape[0]):
        column = grad_first * signs_ref[:, expert : expert + 1]
        grad_normed += column * router_ref[expert : expert + 1, :].astype(jnp.float32)
    grad_scaled = grad_normed * gain_ref[...]
    mean = jnp.mean(grad_scaled * floats, axis=1, keepdims=True)
    grads_ref[...] = (
        cotangent_ref[...].astype(jnp.float32) + inv * grad_scaled - floats * (inv * inv * inv) * mean
    ).astype(jnp.bfloat16)


def swap(value, axis):
    size = lax.axis_size(axis)
    return lax.ppermute(value, axis, [(i, i ^ 1) for i in range(size)])


def sum_over(value, axis):
    size = lax.axis_size(axis)
    if size == 1:
        return value, jnp.zeros_like(value)
    if size == 2:
        return value, swap(value, axis)
    total = lax.psum(value.astype(jnp.float32), axis)
    return total.astype(value.dtype), jnp.zeros_like(value)


def trade(blocks):
    size = len(blocks)
    pairs = [[(i, i ^ step) for i in range(size)] for step in range(size)]
    return [blocks[0]] + [lax.ppermute(blocks[step], "expert", pairs[step]) for step in range(1, size)]


def trade_whole(rows, copies):
    size = lax.axis_size("expert")
    width = rows.shape[1]
    if copies > 1:
        rows = rows.reshape(size // copies, 1, -1, width)
        rows = jnp.broadcast_to(rows, (size // copies, copies) + rows.shape[2:])
    rows = rows.reshape(size, -1, width)
    return lax.all_to_all(rows, "expert", split_axis=0, concat_axis=0, tiled=True).reshape(-1, width)


def layer(tokens, cotangent, gain, w_router, w_gate, w_up, w_down, expert_ids, slots):
    bf16, f32 = jnp.bfloat16, jnp.float32
    experts = w_router.shape[1]
    axis = lax.axis_size("expert")
    copies = axis // experts
    token_count, width = tokens.shape
    rows = 2 * token_count
    capacity = rows // experts
    hidden = w_gate.shape[2]
    parts = 2 if lax.axis_size("dp") % 2 == 0 and hidden % 256 == 0 else 1
    inner = hidden // parts
    paired = copies == 1 and axis in (2, 4, 8) and capacity % 8 == 0
    places = jnp.stack([lax.axis_index("expert"), lax.axis_index("dp") & (parts - 1)]).astype(jnp.int32)
    gain_row = gain.reshape(1, width)
    router = w_router.T
    count = axis * capacity
    all_rows = parts * count
    in_hbm = lambda value: pltpu.with_memory_space_constraint(value, pltpu.HBM)

    sends = [shape((2 * capacity, width), bf16)] * experts if paired else [shape((rows, width), bf16)] * 2
    small = shape((token_count, 128), f32)
    *blocks, first, second, probs, inv, signs, normed, tokens_here, cotangent_here, gain_here, router_here = call(
        functools.partial(prepare, experts, capacity, paired),
        (places, *(in_hbm(v) for v in (expert_ids.T, slots.T, tokens, cotangent, gain_row, router))),
        [SMEM] + [HBM] * 6,
        sends
        + [shape((rows, token_count), bf16)] * 2
        + [small, small, small, shape((token_count, width), bf16)]
        + [pltpu.VMEM((token_count, width), bf16)] * 2
        + [pltpu.VMEM((1, width), f32), pltpu.VMEM((experts, width), bf16)],
        [
            pltpu.VMEM((2, token_count), jnp.int32),
            pltpu.VMEM((2, token_count), jnp.int32),
            pltpu.SemaphoreType.DMA((6,)),
        ],
    )
    blocks = trade(blocks) if paired else [trade_whole(block, copies) for block in blocks]
    (gate_here,) = call(
        fetch,
        (places, in_hbm(w_gate[0])),
        [SMEM, HBM],
        [pltpu.VMEM((width, inner), bf16)],
        [pltpu.SemaphoreType.DMA((1,))],
        limit=1,
        flops=10**10,
        moved=2 * width * inner,
    )
    if parts == 2:
        others = [swap(block, "dp") for block in blocks]
    else:
        others = []
    if paired:
        inputs = grads = blocks + others
    else:
        inputs, grads = blocks[:1] + others[:1], blocks[1:] + others[1:]
    pieces = len(inputs)
    height = piece(inner)
    act, slope, silu, scaled, up_here = call(
        functools.partial(forward, pieces, paired),
        (places, *inputs, gain_here, gate_here, in_hbm(w_up[0])),
        [SMEM] + [VMEM] * (pieces + 2) + [HBM],
        [
            shape((all_rows, inner), bf16),
            shape((inner, all_rows), f32),
            shape((inner, all_rows), f32),
            shape((all_rows, width), f32),
            pltpu.VMEM((width, inner), bf16),
        ],
        [pltpu.SemaphoreType.DMA((inner // height,))],
        limit=4,
        flops=4 * all_rows * width * inner,
        moved=4 * width * inner,
    )
    value_shapes = [shape((count, width), f32)] + [shape((count, width), bf16)] * (parts - 1)
    *values, gate_grad, up_grad = call(
        functools.partial(middle, pieces, paired),
        (places, act, slope, silu, in_hbm(w_down[0]), *grads),
        [SMEM] + [VMEM] * 3 + [HBM] + [VMEM] * pieces,
        value_shapes + [shape((inner, all_rows), bf16)] * 2,
        [
            pltpu.VMEM((all_rows, width), f32),
            pltpu.VMEM((min(MIDDLE_FLIGHT + 1, inner // height), height, width), bf16),
            pltpu.SemaphoreType.DMA((min(MIDDLE_FLIGHT + 1, inner // height),)),
        ],
        limit=10,
        flops=4 * all_rows * width * inner,
        moved=2 * width * inner,
    )
    *backs, gain_part = call(
        backward,
        (gate_grad, up_grad, gate_here, up_here, scaled),
        [VMEM] * 5,
        value_shapes + [shape((1, width), f32)],
        flops=4 * all_rows * width * inner,
        moved=4 * width * inner,
    )
    home_shapes = [shape((capacity, width), bf16)] * experts if paired else [shape((count, width), bf16)]

    def home(pieces):
        if parts == 2:
            mine = call(add_pair, (pieces[0], swap(pieces[1], "dp")), [VMEM] * 2, home_shapes)
        else:
            mine = call(round_own, (pieces[0],), [VMEM], home_shapes)
        if paired:
            return trade(mine)
        back = trade_whole(mine[0], 1)
        if copies > 1:
            back = back.reshape(experts, copies, -1, width).astype(f32)
            back = jnp.sum(back, axis=1).reshape(-1, width).astype(bf16)
        return [back]

    axes = ("dp", "expert", "tensor")
    devices = lax.axis_size(axes)
    tiles = (experts + 1) * (width // 128)
    joint = paired and parts == 2 and capacity == 8 and lax.axis_size("tensor") == 2 and lax.axis_size("dp") == 4
    if joint:
        sums_shape = (capacity, -(-tiles // capacity) * 128)
    else:
        each = -(-tiles // devices)
        sums_shape = (devices * each, 128)
    value_rows = home(values)
    mix, sums = call(
        mix_values,
        (first, second, probs, inv, signs, normed, tokens_here, cotangent_here, router_here, gain_part, *value_rows),
        [VMEM] * (10 + len(value_rows)),
        [shape((token_count, width + 128), bf16), shape(sums_shape, f32)],
    )
    mix, other_mix = sum_over(mix, "tensor")
    last_inputs = (tokens_here, cotangent_here, gain_here, router_here, probs, inv, signs)
    token_shape = shape((token_count, width), bf16)
    router_shapes = [shape((experts, width), f32), shape((1, width), f32)]
    if joint:
        total = sums_shape[1]
        half = -(-total // 256) * 128
        other_backs = swap(backs[1], "dp")
        other_sums = swap(sums, "dp")
        mine = call(
            add_all,
            (backs[0], other_backs, sums, other_sums),
            [VMEM] * 4,
            [shape((capacity, width + total), bf16)] * experts,
        )
        back_rows = trade(mine)
        back, sums, mixed, score = call(
            sum_all,
            (first, second, tokens_here, mix, other_mix, *back_rows),
            [VMEM] * (5 + len(back_rows)),
            [shape((token_count, width + half), bf16), shape(sums_shape, bf16), token_shape, small],
        )
        other_back = swap(back, "tensor")
        side = lax.ppermute(sums, "dp", [(i, i ^ 2) for i in range(4)])
        corner = lax.ppermute(sums, ("dp", "tensor"), [(i, i ^ 5) for i in range(8)])
        grad_tokens, grad_router, grad_gain = call(
            functools.partial(finish, True),
            (*last_inputs, back, other_back, score, sums, side, corner),
            [VMEM] * 13,
            [token_shape] + router_shapes,
        )
        return (mixed, grad_tokens, grad_router.T, grad_gain.reshape(width))
    back_rows = home(backs)
    (back,) = call(
        sum_rows, (first, second, *back_rows), [VMEM] * (2 + len(back_rows)), [shape((token_count, width), bf16)]
    )
    back, other_back = sum_over(back, "tensor")
    mixed, grad_tokens = call(
        functools.partial(finish, False),
        (*last_inputs, back, other_back, mix, other_mix),
        [VMEM] * 11,
        [token_shape] * 2,
    )
    sums = sums.reshape(devices, each, 128)
    sums = lax.all_to_all(sums, axes, split_axis=0, concat_axis=0, tiled=True)
    sums = jnp.broadcast_to(jnp.sum(sums, axis=0, keepdims=True), sums.shape)
    sums = lax.all_to_all(sums, axes, split_axis=0, concat_axis=0, tiled=True)
    sums = sums.reshape(devices * each, 128)
    grad_router, grad_gain = call(gather_sums, (sums,), [VMEM], router_shapes)
    return (mixed, grad_tokens, grad_router.T, grad_gain.reshape(width))


def solution(mesh):
    return jax.shard_map(
        layer,
        mesh=mesh,
        in_specs=(
            P(("dp", "expert"), None),
            P(("dp", "expert"), None),
            P(),
            P(),
            P("expert", None, "tensor"),
            P("expert", None, "tensor"),
            P("expert", "tensor", None),
            P(("dp", "expert"), None),
            P(("dp", "expert"), None),
        ),
        out_specs=(P(("dp", "expert"), None), P(("dp", "expert"), None), P(), P()),
        check_vma=False,
    )
```

time: 107 us -> 79.3 us (0.74)
  local copies, waits for them, and re-layouts: 19.6 us -> 0 us
  starting transfers between devices: 32.1 us -> 21.2 us
  waiting for transfers between devices: 17.4 us -> 21.3 us
    unnamed x25 -> x0, local copies, waits for them, and re-layouts: 16.8 us -> none
    ppermute x12 -> x9, waiting for transfers between devices: 9.01 us -> 17.9 us  [trade(): lax.ppermute(blocks[step], 'expert', pairs[step])]
    all_to_all x2 -> x0, starting transfers between devices: 7.33 us -> none  [the longest x1 4.42 us: all_sum(): mine = lax.all_to_all(blocks, axes, split_axis=0, concat_axis=0, tiled=True)]
    ppermute x13 -> x9, waiting for transfers between devices: 4.74 us -> 0.02 us  [swap(): return lax.ppermute(value, axis, [(i, i ^ 1) for i in range(size)])]
    ppermute x12 -> x9, starting transfers between devices: 19.1 us -> 14.6 us  [trade(): lax.ppermute(blocks[step], 'expert', pairs[step])]
    all_to_all x2 -> x0, waiting for transfers between devices: 3.66 us -> none  [the longest x1 2.93 us: all_sum(): mine = lax.all_to_all(blocks, axes, split_axis=0, concat_axis=0, tiled=True)]
    ppermute x0 -> x2, waiting for transfers between devices: none -> 3.39 us  [the longest x1 2.77 us: layer(): lax.ppermute(sums, ('dp', 'tensor'), [(i, i ^ 5) for i in range(8)])]
    ppermute x0 -> x2, starting transfers between devices: none -> 2.32 us  [the longest x1 1.82 us: layer(): lax.ppermute(sums, ('dp', 'tensor'), [(i, i ^ 5) for i in range(8)])]
  transfers between devices with their start and end apart: 27 -> 20, of which waited for: 9 -> 8; matrix products, arithmetic and copies ran while one was open for 2% -> 0% of each run, Pallas kernels for 22% -> 18%
where the time goes in v2:
time: 79.3 us; the launch traced here: 79.1 us
  Pallas kernels  35.8 us (45%)
  waiting for transfers between devices  21.3 us (27%)
  starting transfers between devices  21.2 us (27%)
    pallas_call x10, Pallas kernels, call(): pl.pallas_call(body, in_specs=in_specs, out_specs=[VMEM] * len(outs), out...  35.8 us
    ppermute x9, waiting for transfers between devices, trade(): lax.ppermute(blocks[step], 'expert', pairs[step])  17.9 us
    ppermute x9, starting transfers between devices, trade(): lax.ppermute(blocks[step], 'expert', pairs[step])  14.6 us
    ppermute x9, starting transfers between devices, swap(): return lax.ppermute(value, axis, [(i, i ^ 1) for i in range(size)])  4.25 us
    ppermute x1, waiting for transfers between devices, layer(): lax.ppermute(sums, ('dp', 'tensor'), [(i, i ^ 5) for i in range(8)])  2.77 us
    ppermute x1, starting transfers between devices, layer(): lax.ppermute(sums, ('dp', 'tensor'), [(i, i ^ 5) for i in range(8)])  1.82 us
  transfers between devices with their start and end apart: 20, of which 8 were waited for; matrix products, arithmetic and copies ran while one was open for 0% of the time, Pallas kernels for 18%

profile of v2, /device:TPU:0, one launch (start us, length us, event | category | flops | bytes accessed | tf_op | source)
XLA Modules:
  0.0 79.1 jit_solution(12970738821172771183)
XLA Ops:
  0.6 0.1 pad_add_fusion.places_ref
  0.7 2.0 %shard_map.120 = (bf16[16,3072]{1,0:T(8,128)(2,1)S(1)}, bf16[16,3072]{1,0:T(8,128)(2,1)S(1)}, bf16[16,3072]{1,0:T(8,128)(2,1)S(1)}, bf16[16,3072]{1,0:T(8,128)(2...) custom-call(s32[2]{0:T(128)S(1)} %pad_add_fusion.places_ref, ...), custom_call_target="tpu_custom_call" | custom-call | tf_op jit(solution)/shard_map/pallas_call | solution.py:30
  2.7 3.1 %collective-permute-start = (bf16[16,3072]{1,0:T(8,128)(2,1)S(1)}, bf16[16,3072]{1,0:T(8,128)(2,1)S(1)}, u32[]{:S(2)}, u32[]{:S(2)}) collective-permute-start(bf16[16,3072]{1,0:T(8,128)(2,1)S(1)} %get-tuple-element.57), channel_id=1, source_target_pairs={{0,2},{2,0},{4,6},{6,4},{1,3},{3,1},{5,7},{7,5},{8,10},{10,8},{12,... | collective-permute-start | bytes 294920 | tf_op jit(solution)/shard_map/ppermute | solution.py:371
  5.9 2.6 %collective-permute-start.1 = (bf16[16,3072]{1,0:T(8,128)(2,1)S(1)}, bf16[16,3072]{1,0:T(8,128)(2,1)S(1)}, u32[]{:S(2)}, u32[]{:S(2)}) collective-permute-start(bf16[16,3072]{1,0:T(8,128)(2,1)S(1)} %get-tuple-element.58), channel_id=1, source_target_pairs={{0,4},{2,6},{4,0},{6,2},{1,5},{3,7},{5,1},{7,3},{8,12},{10,14},{12... | collective-permute-start | bytes 294920 | tf_op jit(solution)/shard_map/ppermute | solution.py:371
  8.4 0.0 collective-permute-start.2
  8.5 0.0 collective-permute-start.3
  8.5 0.2 collective-permute-done.refs_1_
  8.7 0.3 collective-permute-start.4
  9.0 7.3 %collective-permute-done.1.refs_2_ = bf16[16,3072]{1,0:T(8,128)(2,1)S(1)} collective-permute-done((bf16[16,3072]{1,0:T(8,128)(2,1)S(1)}, bf16[16,3072]{1,0:T(8,128)(2,1)S(1)}, u32[]{:S(2)}, u32[]{:S(2)}) %collective-permute-start.1) | collective-permute-done | bytes 98336 | tf_op jit(solution)/shard_map/ppermute | solution.py:371
  16.3 0.0 collective-permute-start.5
  16.3 0.0 collective-permute-done.2.refs_3_
  16.3 0.5 collective-permute-start.6
  16.8 5.6 %shard_map.121.refs_9_.gate_ref = bf16[3072,2304]{1,0:T(8,128)(2,1)S(1)} custom-call(s32[2]{0:T(128)S(1)} %pad_add_fusion.places_ref, bf16[3072,4608]{1,0:T(8,128)(2,1)} %bitcast.13), custom_call_target="tpu_custom_call" | custom-call | flops 10000000000 | bytes 14155776 | tf_op jit(solution)/shard_map/pallas_call | solution.py:30
  22.4 0.0 collective-permute-done.3.refs_4_
  22.4 0.0 collective-permute-done.4.refs_5_
  22.4 0.0 collective-permute-done.5.refs_6_
  22.4 0.0 collective-permute-done.6.refs_7_
  22.4 9.2 %shard_map.122 = (bf16[64,2304]{1,0:T(8,128)(2,1)S(1)}, f32[2304,64]{1,0:T(8,128)S(1)}, f32[2304,64]{1,0:T(8,128)S(1)}, f32[64,3072]{1,0:T(8,128)S(1)}, bf16[3072,2304]{1,0:T(8,128)(2,1)S(1)}) custom-call(s32[2]{0:T(128)S(1)} %pad_add_fusion.places_ref, bf16[16,3072]{1,0:T(8,128)(2,1)S(1)} %get-tuple-element.56.refs_0_, ...), custom_call_target="tpu_custom_call" | custom-call | flops 1811939328 | bytes 28311552 | tf_op jit(solution)/shard_map/pallas_call | solution.py:30
  31.6 8.6 %shard_map.123 = (f32[32,3072]{1,0:T(8,128)S(1)}, bf16[32,3072]{1,0:T(8,128)(2,1)S(1)}, bf16[2304,64]{1,0:T(8,128)(2,1)S(1)}, bf16[2304,64]{1,0:T(8,128)(2,1)S(1)}) custom-call(s32[2]{0:T(128)S(1)} %pad_add_fusion.places_ref, bf16[64,2304]{1,0:T(8,128)(2,1)S(1)} %get-tuple-element.61.act_ref, f32[2304,64]{1,0:T(8,128)S(1)} %get-tuple-element.62.slope_ref, ...), custom_call_target="tpu_custom_call" | custom-call | flops 1811939328 | bytes 14155776 | tf_op jit(solution)/shard_map/pallas_call | solution.py:30
  40.2 0.1 collective-permute-start.7
  40.3 7.9 %shard_map.124 = (f32[32,3072]{1,0:T(8,128)S(1)}, bf16[32,3072]{1,0:T(8,128)(2,1)S(1)}, f32[1,3072]{1,0:T(1,128)S(1)}) custom-call(bf16[2304,64]{1,0:T(8,128)(2,1)S(1)} %get-tuple-element.64.gate_grad_ref, bf16[2304,64]{1,0:T(8,128)(2,1)S(1)} %get-tuple-element.65.up_grad_ref, bf16[3072,2304]{1,0:T(8,128)(2,1)S(1)} %shard_map.121.refs_9_.gate_ref, ...), custom_call_target="tpu_custom_call" | custom-call | flops 1811939328 | bytes 28311552 | tf_op jit(solution)/shard_map/pallas_call | solution.py:30
  48.2 0.6 collective-permute-start.12
  48.8 0.0 collective-permute-done.7.other_ref
  48.8 1.2 %collective-permute-start.8 = (bf16[8,3072]{1,0:T(8,128)(2,1)S(1)}, bf16[8,3072]{1,0:T(8,128)(2,1)S(1)}, u32[]{:S(2)}, u32[]{:S(2)}) collective-permute-start(bf16[8,3072]{1,0:T(8,128)(2,1)S(1)} %get-tuple-element.72), channel_id=1, source_target_pairs={{0,2},{2,0},{4,6},{6,4},{1,3},{3,1},{5,7},{7,5},{8,10},{10,8},{12,... | collective-permute-start | bytes 147464 | tf_op jit(solution)/shard_map/ppermute | solution.py:371
  50.0 1.9 %collective-permute-start.9 = (bf16[8,3072]{1,0:T(8,128)(2,1)S(1)}, bf16[8,3072]{1,0:T(8,128)(2,1)S(1)}, u32[]{:S(2)}, u32[]{:S(2)}) collective-permute-start(bf16[8,3072]{1,0:T(8,128)(2,1)S(1)} %get-tuple-element.73), channel_id=1, source_target_pairs={{0,4},{2,6},{4,0},{6,2},{1,5},{3,7},{5,1},{7,3},{8,12},{10,14},{12... | collective-permute-start | bytes 147464 | tf_op jit(solution)/shard_map/ppermute | solution.py:371
  51.9 1.3 %collective-permute-start.10 = (bf16[8,3072]{1,0:T(8,128)(2,1)S(1)}, bf16[8,3072]{1,0:T(8,128)(2,1)S(1)}, u32[]{:S(2)}, u32[]{:S(2)}) collective-permute-start(bf16[8,3072]{1,0:T(8,128)(2,1)S(1)} %get-tuple-element.74), channel_id=1, source_target_pairs={{0,6},{2,4},{4,2},{6,0},{1,7},{3,5},{5,3},{7,1},{8,14},{10,12},{12... | collective-permute-start | bytes 147464 | tf_op jit(solution)/shard_map/ppermute | solution.py:371
  53.3 0.0 collective-permute-done.8.refs_1_
  53.3 3.4 %collective-permute-done.9.refs_2_ = bf16[8,3072]{1,0:T(8,128)(2,1)S(1)} collective-permute-done((bf16[8,3072]{1,0:T(8,128)(2,1)S(1)}, bf16[8,3072]{1,0:T(8,128)(2,1)S(1)}, u32[]{:S(2)}, u32[]{:S(2)}) %collective-permute-start.9) | collective-permute-done | bytes 49184 | tf_op jit(solution)/shard_map/ppermute | solution.py:371
  56.6 1.3 %collective-permute-done.10.refs_3_ = bf16[8,3072]{1,0:T(8,128)(2,1)S(1)} collective-permute-done((bf16[8,3072]{1,0:T(8,128)(2,1)S(1)}, bf16[8,3072]{1,0:T(8,128)(2,1)S(1)}, u32[]{:S(2)}, u32[]{:S(2)}) %collective-permute-start.10) | collective-permute-done | bytes 49184 | tf_op jit(solution)/shard_map/ppermute | solution.py:371
  57.9 0.7 shard_map.126
  58.6 0.1 collective-permute-start.13
  58.7 1.6 %collective-permute-start.11 = (bf16[16,3200]{1,0:T(8,128)(2,1)S(1)}, bf16[16,3200]{1,0:T(8,128)(2,1)S(1)}, u32[]{:S(2)}, u32[]{:S(2)}) collective-permute-start(bf16[16,3200]{1,0:T(8,128)(2,1)S(1)} %get-tuple-element.75.mix_ref), channel_id=1, source_target_pairs={{0,1},{1,0},{2,3},{3,2},{4,5},{5,4},{6,7},{7,6},{8,9},{9,8},{10,11... | collective-permute-start | bytes 307208 | tf_op jit(solution)/shard_map/ppermute | solution.py:355
  60.2 0.0 collective-permute-done.12.other_ref
  60.2 0.0 collective-permute-done.13.other_sums_ref
  60.2 0.1 shard_map.127
  60.3 0.7 collective-permute-start.14
  61.0 1.6 %collective-permute-start.15 = (bf16[8,4992]{1,0:T(8,128)(2,1)S(1)}, bf16[8,4992]{1,0:T(8,128)(2,1)S(1)}, u32[]{:S(2)}, u32[]{:S(2)}) collective-permute-start(bf16[8,4992]{1,0:T(8,128)(2,1)S(1)} %get-tuple-element.81), channel_id=1, source_target_pairs={{0,4},{2,6},{4,0},{6,2},{1,5},{3,7},{5,1},{7,3},{8,12},{10,14},{12... | collective-permute-start | bytes 239624 | tf_op jit(solution)/shard_map/ppermute | solution.py:371
  62.6 2.1 %collective-permute-start.16 = (bf16[8,4992]{1,0:T(8,128)(2,1)S(1)}, bf16[8,4992]{1,0:T(8,128)(2,1)S(1)}, u32[]{:S(2)}, u32[]{:S(2)}) collective-permute-start(bf16[8,4992]{1,0:T(8,128)(2,1)S(1)} %get-tuple-element.82), channel_id=1, source_target_pairs={{0,6},{2,4},{4,2},{6,0},{1,7},{3,5},{5,3},{7,1},{8,14},{10,12},{12... | collective-permute-start | bytes 239624 | tf_op jit(solution)/shard_map/ppermute | solution.py:371
  64.7 0.0 collective-permute-done.11.other_mix_ref
  64.7 1.0 %collective-permute-done.14.refs_1_ = bf16[8,4992]{1,0:T(8,128)(2,1)S(1)} collective-permute-done((bf16[8,4992]{1,0:T(8,128)(2,1)S(1)}, bf16[8,4992]{1,0:T(8,128)(2,1)S(1)}, u32[]{:S(2)}, u32[]{:S(2)}) %collective-permute-start.14) | collective-permute-done | bytes 79904 | tf_op jit(solution)/shard_map/ppermute | solution.py:371
  65.7 4.7 %collective-permute-done.15.refs_2_ = bf16[8,4992]{1,0:T(8,128)(2,1)S(1)} collective-permute-done((bf16[8,4992]{1,0:T(8,128)(2,1)S(1)}, bf16[8,4992]{1,0:T(8,128)(2,1)S(1)}, u32[]{:S(2)}, u32[]{:S(2)}) %collective-permute-start.15) | collective-permute-done | bytes 79904 | tf_op jit(solution)/shard_map/ppermute | solution.py:371
  70.4 0.0 collective-permute-done.16.refs_3_
  70.4 0.8 %shard_map.128 = (bf16[16,4096]{1,0:T(8,128)(2,1)S(1)}, bf16[8,1920]{1,0:T(8,128)(2,1)S(1)}, bf16[16,3072]{1,0:T(8,128)(2,1)}, f32[16,128]{1,0:T(8,128)S(1)}) custom-call(bf16[32,16]{1,0:T(8,128)(2,1)S(1)} %get-tuple-element.47.first_ref, bf16[32,16]{1,0:T(8,128)(2,1)S(1)} %get-tuple-element.48.second_ref, ...), custom_call_target="tpu_custom_call" | custom-call | tf_op jit(solution)/shard_map/pallas_call | solution.py:30
  71.2 1.2 %collective-permute-start.17 = (bf16[16,4096]{1,0:T(8,128)(2,1)S(1)}, bf16[16,4096]{1,0:T(8,128)(2,1)S(1)}, u32[]{:S(2)}, u32[]{:S(2)}) collective-permute-start(bf16[16,4096]{1,0:T(8,128)(2,1)S(1)} %get-tuple-element.84.back_ref), channel_id=1, source_target_pairs={{0,1},{1,0},{2,3},{3,2},{4,5},{5,4},{6,7},{7,6},{8,9},{9,8},{10,11... | collective-permute-start | bytes 393224 | tf_op jit(solution)/shard_map/ppermute | solution.py:355
  72.4 1.8 %collective-permute-start.19 = (bf16[8,1920]{1,0:T(8,128)(2,1)S(1)}, bf16[8,1920]{1,0:T(8,128)(2,1)S(1)}, u32[]{:S(2)}, u32[]{:S(2)}) collective-permute-start(bf16[8,1920]{1,0:T(8,128)(2,1)S(1)} %get-tuple-element.86.refs_1_), channel_id=1, source_target_pairs={{0,17},{1,16},{8,25},{9,24},{16,1},{17,0},{24,9},{25,8},{2,19},{3,... | collective-permute-start | bytes 92168 | tf_op jit(solution)/shard_map/ppermute | solution.py:535
  74.2 0.5 collective-permute-start.18
  74.7 2.8 %collective-permute-done.19.refs_3_ = bf16[8,1920]{1,0:T(8,128)(2,1)S(1)} collective-permute-done((bf16[8,1920]{1,0:T(8,128)(2,1)S(1)}, bf16[8,1920]{1,0:T(8,128)(2,1)S(1)}, u32[]{:S(2)}, u32[]{:S(2)}) %collective-permute-start.19) | collective-permute-done | bytes 30752 | tf_op jit(solution)/shard_map/ppermute | solution.py:535
  77.5 0.6 collective-permute-done.18.refs_2_
  78.1 0.0 collective-permute-done.17.other_back_ref
  78.1 1.0 %shard_map.129 = (bf16[16,3072]{1,0:T(8,128)(2,1)}, f32[4,3072]{1,0:T(4,128)}, f32[1,3072]{1,0:T(1,128)}) custom-call(bf16[16,3072]{1,0:T(8,128)(2,1)S(1)} %get-tuple-element.49.tokens_ref, bf16[16,3072]{1,0:T(8,128)(2,1)S(1)} %get-tuple-element.54.cotangent_ref, f32[1,3072]{1,0:T(1,128)S(1)} %get-tuple-element.60.refs_8_.gain_ref, ...), custom_call_target="tpu_custom_call" | custom-call | tf_op jit(solution)/shard_map/pallas_call | solution.py:30
  (1 shorter events, 0.0 us)
Async XLA Ops:
  2.7 5.9 %collective-permute-start = (bf16[16,3072]{1,0:T(8,128)(2,1)S(1)}, bf16[16,3072]{1,0:T(8,128)(2,1)S(1)}, u32[]{:S(2)}, u32[]{:S(2)}) collective-permute-start(bf16[16,3072]{1,0:T(8,128)(2,1)S(1)} %get-tuple-element.57), channel_id=1, source_target_pairs={{0,2},{2,0},{4,6},{6,4},{1,3},{3,1},{5,7},{7,5},{8,10},{10,8},{12,... | collective-permute-start | bytes 294920 | tf_op jit(solution)/shard_map/ppermute | solution.py:371
  5.9 10.4 %collective-permute-start.1 = (bf16[16,3072]{1,0:T(8,128)(2,1)S(1)}, bf16[16,3072]{1,0:T(8,128)(2,1)S(1)}, u32[]{:S(2)}, u32[]{:S(2)}) collective-permute-start(bf16[16,3072]{1,0:T(8,128)(2,1)S(1)} %get-tuple-element.58), channel_id=1, source_target_pairs={{0,4},{2,6},{4,0},{6,2},{1,5},{3,7},{5,1},{7,3},{8,12},{10,14},{12... | collective-permute-start | bytes 294920 | tf_op jit(solution)/shard_map/ppermute | solution.py:371
  8.4 7.8 %collective-permute-start.2 = (bf16[16,3072]{1,0:T(8,128)(2,1)S(1)}, bf16[16,3072]{1,0:T(8,128)(2,1)S(1)}, u32[]{:S(2)}, u32[]{:S(2)}) collective-permute-start(bf16[16,3072]{1,0:T(8,128)(2,1)S(1)} %get-tuple-element.59), channel_id=1, source_target_pairs={{0,6},{2,4},{4,2},{6,0},{1,7},{3,5},{5,3},{7,1},{8,14},{10,12},{12... | collective-permute-start | bytes 294920 | tf_op jit(solution)/shard_map/ppermute | solution.py:371
  8.5 13.9 %collective-permute-start.3 = (bf16[16,3072]{1,0:T(8,128)(2,1)S(1)}, bf16[16,3072]{1,0:T(8,128)(2,1)S(1)}, u32[]{:S(2)}, u32[]{:S(2)}) collective-permute-start(bf16[16,3072]{1,0:T(8,128)(2,1)S(1)} %get-tuple-element.56.refs_0_), channel_id=1, source_target_pairs={{0,8},{8,0},{16,24},{24,16},{1,9},{9,1},{17,25},{25,17},{2,10},{10... | collective-permute-start | bytes 294920 | tf_op jit(solution)/shard_map/ppermute | solution.py:355
  8.7 13.7 %collective-permute-start.4 = (bf16[16,3072]{1,0:T(8,128)(2,1)S(1)}, bf16[16,3072]{1,0:T(8,128)(2,1)S(1)}, u32[]{:S(2)}, u32[]{:S(2)}) collective-permute-start(bf16[16,3072]{1,0:T(8,128)(2,1)S(1)} %collective-permute-done.refs_1_), channel_id=1, source_target_pairs={{0,8},{8,0},{16,24},{24,16},{1,9},{9,1},{17,25},{25,17},{2,10},{10... | collective-permute-start | bytes 294920 | tf_op jit(solution)/shard_map/ppermute | solution.py:355
  16.3 6.1 %collective-permute-start.5 = (bf16[16,3072]{1,0:T(8,128)(2,1)S(1)}, bf16[16,3072]{1,0:T(8,128)(2,1)S(1)}, u32[]{:S(2)}, u32[]{:S(2)}) collective-permute-start(bf16[16,3072]{1,0:T(8,128)(2,1)S(1)} %collective-permute-done.1.refs_2_), channel_id=1, source_target_pairs={{0,8},{8,0},{16,24},{24,16},{1,9},{9,1},{17,25},{25,17},{2,10},{10... | collective-permute-start | bytes 294920 | tf_op jit(solution)/shard_map/ppermute | solution.py:355
  16.3 6.1 %collective-permute-start.6 = (bf16[16,3072]{1,0:T(8,128)(2,1)S(1)}, bf16[16,3072]{1,0:T(8,128)(2,1)S(1)}, u32[]{:S(2)}, u32[]{:S(2)}) collective-permute-start(bf16[16,3072]{1,0:T(8,128)(2,1)S(1)} %collective-permute-done.2.refs_3_), channel_id=1, source_target_pairs={{0,8},{8,0},{16,24},{24,16},{1,9},{9,1},{17,25},{25,17},{2,10},{10... | collective-permute-start | bytes 294920 | tf_op jit(solution)/shard_map/ppermute | solution.py:355
  40.2 8.6 %collective-permute-start.7 = (bf16[32,3072]{1,0:T(8,128)(2,1)S(1)}, bf16[32,3072]{1,0:T(8,128)(2,1)S(1)}, u32[]{:S(2)}, u32[]{:S(2)}) collective-permute-start(bf16[32,3072]{1,0:T(8,128)(2,1)S(1)} %get-tuple-element.70), channel_id=1, source_target_pairs={{0,8},{8,0},{16,24},{24,16},{1,9},{9,1},{17,25},{25,17},{2,10},{10... | collective-permute-start | bytes 589832 | tf_op jit(solution)/shard_map/ppermute | solution.py:355
  48.2 12.0 %collective-permute-start.12 = (bf16[32,3072]{1,0:T(8,128)(2,1)S(1)}, bf16[32,3072]{1,0:T(8,128)(2,1)S(1)}, u32[]{:S(2)}, u32[]{:S(2)}) collective-permute-start(bf16[32,3072]{1,0:T(8,128)(2,1)S(1)} %get-tuple-element.77), channel_id=1, source_target_pairs={{0,8},{8,0},{16,24},{24,16},{1,9},{9,1},{17,25},{25,17},{2,10},{10... | collective-permute-start | bytes 589832 | tf_op jit(solution)/shard_map/ppermute | solution.py:355
  48.8 4.5 %collective-permute-start.8 = (bf16[8,3072]{1,0:T(8,128)(2,1)S(1)}, bf16[8,3072]{1,0:T(8,128)(2,1)S(1)}, u32[]{:S(2)}, u32[]{:S(2)}) collective-permute-start(bf16[8,3072]{1,0:T(8,128)(2,1)S(1)} %get-tuple-element.72), channel_id=1, source_target_pairs={{0,2},{2,0},{4,6},{6,4},{1,3},{3,1},{5,7},{7,5},{8,10},{10,8},{12,... | collective-permute-start | bytes 147464 | tf_op jit(solution)/shard_map/ppermute | solution.py:371
  50.0 6.6 %collective-permute-start.9 = (bf16[8,3072]{1,0:T(8,128)(2,1)S(1)}, bf16[8,3072]{1,0:T(8,128)(2,1)S(1)}, u32[]{:S(2)}, u32[]{:S(2)}) collective-permute-start(bf16[8,3072]{1,0:T(8,128)(2,1)S(1)} %get-tuple-element.73), channel_id=1, source_target_pairs={{0,4},{2,6},{4,0},{6,2},{1,5},{3,7},{5,1},{7,3},{8,12},{10,14},{12... | collective-permute-start | bytes 147464 | tf_op jit(solution)/shard_map/ppermute | solution.py:371
  51.9 6.0 %collective-permute-start.10 = (bf16[8,3072]{1,0:T(8,128)(2,1)S(1)}, bf16[8,3072]{1,0:T(8,128)(2,1)S(1)}, u32[]{:S(2)}, u32[]{:S(2)}) collective-permute-start(bf16[8,3072]{1,0:T(8,128)(2,1)S(1)} %get-tuple-element.74), channel_id=1, source_target_pairs={{0,6},{2,4},{4,2},{6,0},{1,7},{3,5},{5,3},{7,1},{8,14},{10,12},{12... | collective-permute-start | bytes 147464 | tf_op jit(solution)/shard_map/ppermute | solution.py:371
  58.6 1.6 %collective-permute-start.13 = (f32[8,1920]{1,0:T(8,128)S(1)}, f32[8,1920]{1,0:T(8,128)S(1)}, u32[]{:S(2)}, u32[]{:S(2)}) collective-permute-start(f32[8,1920]{1,0:T(8,128)S(1)} %get-tuple-element.78.sums_ref), channel_id=1, source_target_pairs={{0,8},{8,0},{16,24},{24,16},{1,9},{9,1},{17,25},{25,17},{2,10},{10... | collective-permute-start | bytes 184328 | tf_op jit(solution)/shard_map/ppermute | solution.py:355
  58.7 6.1 %collective-permute-start.11 = (bf16[16,3200]{1,0:T(8,128)(2,1)S(1)}, bf16[16,3200]{1,0:T(8,128)(2,1)S(1)}, u32[]{:S(2)}, u32[]{:S(2)}) collective-permute-start(bf16[16,3200]{1,0:T(8,128)(2,1)S(1)} %get-tuple-element.75.mix_ref), channel_id=1, source_target_pairs={{0,1},{1,0},{2,3},{3,2},{4,5},{5,4},{6,7},{7,6},{8,9},{9,8},{10,11... | collective-permute-start | bytes 307208 | tf_op jit(solution)/shard_map/ppermute | solution.py:355
  60.3 5.5 %collective-permute-start.14 = (bf16[8,4992]{1,0:T(8,128)(2,1)S(1)}, bf16[8,4992]{1,0:T(8,128)(2,1)S(1)}, u32[]{:S(2)}, u32[]{:S(2)}) collective-permute-start(bf16[8,4992]{1,0:T(8,128)(2,1)S(1)} %get-tuple-element.80), channel_id=1, source_target_pairs={{0,2},{2,0},{4,6},{6,4},{1,3},{3,1},{5,7},{7,5},{8,10},{10,8},{12,... | collective-permute-start | bytes 239624 | tf_op jit(solution)/shard_map/ppermute | solution.py:371
  61.0 9.4 %collective-permute-start.15 = (bf16[8,4992]{1,0:T(8,128)(2,1)S(1)}, bf16[8,4992]{1,0:T(8,128)(2,1)S(1)}, u32[]{:S(2)}, u32[]{:S(2)}) collective-permute-start(bf16[8,4992]{1,0:T(8,128)(2,1)S(1)} %get-tuple-element.81), channel_id=1, source_target_pairs={{0,4},{2,6},{4,0},{6,2},{1,5},{3,7},{5,1},{7,3},{8,12},{10,14},{12... | collective-permute-start | bytes 239624 | tf_op jit(solution)/shard_map/ppermute | solution.py:371
  62.6 7.8 %collective-permute-start.16 = (bf16[8,4992]{1,0:T(8,128)(2,1)S(1)}, bf16[8,4992]{1,0:T(8,128)(2,1)S(1)}, u32[]{:S(2)}, u32[]{:S(2)}) collective-permute-start(bf16[8,4992]{1,0:T(8,128)(2,1)S(1)} %get-tuple-element.82), channel_id=1, source_target_pairs={{0,6},{2,4},{4,2},{6,0},{1,7},{3,5},{5,3},{7,1},{8,14},{10,12},{12... | collective-permute-start | bytes 239624 | tf_op jit(solution)/shard_map/ppermute | solution.py:371
  71.2 6.9 %collective-permute-start.17 = (bf16[16,4096]{1,0:T(8,128)(2,1)S(1)}, bf16[16,4096]{1,0:T(8,128)(2,1)S(1)}, u32[]{:S(2)}, u32[]{:S(2)}) collective-permute-start(bf16[16,4096]{1,0:T(8,128)(2,1)S(1)} %get-tuple-element.84.back_ref), channel_id=1, source_target_pairs={{0,1},{1,0},{2,3},{3,2},{4,5},{5,4},{6,7},{7,6},{8,9},{9,8},{10,11... | collective-permute-start | bytes 393224 | tf_op jit(solution)/shard_map/ppermute | solution.py:355
  72.4 5.1 %collective-permute-start.19 = (bf16[8,1920]{1,0:T(8,128)(2,1)S(1)}, bf16[8,1920]{1,0:T(8,128)(2,1)S(1)}, u32[]{:S(2)}, u32[]{:S(2)}) collective-permute-start(bf16[8,1920]{1,0:T(8,128)(2,1)S(1)} %get-tuple-element.86.refs_1_), channel_id=1, source_target_pairs={{0,17},{1,16},{8,25},{9,24},{16,1},{17,0},{24,9},{25,8},{2,19},{3,... | collective-permute-start | bytes 92168 | tf_op jit(solution)/shard_map/ppermute | solution.py:535
  74.2 3.9 %collective-permute-start.18 = (bf16[8,1920]{1,0:T(8,128)(2,1)S(1)}, bf16[8,1920]{1,0:T(8,128)(2,1)S(1)}, u32[]{:S(2)}, u32[]{:S(2)}) collective-permute-start(bf16[8,1920]{1,0:T(8,128)(2,1)S(1)} %get-tuple-element.86.refs_1_), channel_id=1, source_target_pairs={{0,16},{8,24},{16,0},{24,8},{1,17},{9,25},{17,1},{25,9},{2,18},{10... | collective-permute-start | bytes 92168 | tf_op jit(solution)/shard_map/ppermute | solution.py:534

commit v3 on v2

--- a/solution.py
+++ b/solution.py
@@ -40,7 +40,7 @@
 
 def piece(size):
     for width in (256, 128):
-        if size % width == 0:
+        if size % width == 0 and size > width:
             return width
     return size
 
@@ -110,10 +110,14 @@
         signs_ref[:, expert : expert + 1] = column(signs[expert : expert + 1, :])
 
 
-def fetch(places_ref, gate_ref, gate_out, sems):
-    width = gate_out.shape[1]
-    columns = pl.ds(pl.multiple_of(places_ref[1] * width, width), width)
-    load_all(((gate_ref.at[:, columns], gate_out),), sems)
+def fetch(places_ref, gate_ref, up_ref, gate_out, up_out, sems):
+    inner = gate_out.shape[1]
+    early = up_out.shape[1]
+    base = places_ref[1] * inner
+    step = piece(inner)
+    columns = pl.ds(pl.multiple_of(base, step), inner)
+    first = pl.ds(pl.multiple_of(base, step), early)
+    load_all(((gate_ref.at[:, columns], gate_out), (up_ref.at[:, first], up_out)), sems)
 
 
 def stack(refs, paired=False, half=0):
@@ -133,30 +137,36 @@
         ref[...] = value[place * rows : (place + 1) * rows].astype(ref.dtype)
 
 
-MIDDLE_FLIGHT = 3
-
-
 def forward(count, paired, places_ref, *refs):
     tokens_refs = refs[:count]
-    gain_ref, gate_ref, up_any, act_ref, slope_ref, silu_ref, scaled_ref, up_ref, sems = refs[count:]
+    gain_ref, gate_ref, first_ref, up_any = refs[count : count + 4]
+    act_ref, slope_ref, silu_ref, scaled_ref, rest_ref, sems = refs[count + 4 :]
     inner = act_ref.shape[1]
     width = piece(inner)
-    copies = []
-    for step in range(inner // width):
-        there = pl.ds(pl.multiple_of(places_ref[1] * inner + step * width, width), width)
-        here = up_ref.at[:, pl.ds(step * width, width)]
-        copies.append(pltpu.make_async_copy(up_any.at[:, there], here, sems.at[step]))
-        copies[step].start()
+    steps = inner // width
+    early = first_ref.shape[1] // width
+    base = places_ref[1] * inner
+
+    def copy(step):
+        there = pl.ds(pl.multiple_of(base + step * width, width), width)
+        here = rest_ref.at[:, pl.ds((step - early) * width, width)]
+        return pltpu.make_async_copy(up_any.at[:, there], here, sems.at[step - early])
+
+    for step in range(early, steps):
+        copy(step).start()
     floats = stack(tokens_refs, paired, 0)
     inv = lax.rsqrt(jnp.mean(floats * floats, axis=1, keepdims=True) + epsilon)
     scaled = floats * inv
     scaled_ref[...] = scaled
     normed = (scaled * gain_ref[...]).astype(jnp.bfloat16)
-    for step in range(inner // width):
+    for step in range(steps):
         span = pl.ds(step * width, width)
         gate = mm(normed, gate_ref[:, span], NN)
-        copies[step].wait()
-        up = mm(normed, up_ref[:, span], NN)
+        if step < early:
+            up = mm(normed, first_ref[:, span], NN)
+        else:
+            copy(step).wait()
+            up = mm(normed, rest_ref[:, pl.ds((step - early) * width, width)], NN)
         sigmoid = jax.nn.sigmoid(gate)
         silu = gate * sigmoid
         act_ref[:, span] = (silu * up).astype(jnp.bfloat16)
@@ -192,13 +202,15 @@
     split(total_ref[...], value_refs)
 
 
-def backward(gate_grad_ref, up_grad_ref, gate_ref, up_ref, scaled_ref, *refs):
+def backward(gate_grad_ref, up_grad_ref, gate_ref, first_ref, rest_ref, scaled_ref, *refs):
     *value_refs, gain_ref = refs
     rows = value_refs[0].shape[0]
     height = piece(gate_ref.shape[0])
+    early = first_ref.shape[1]
     for start in range(0, gate_ref.shape[0], height):
         span = pl.ds(start, height)
-        back = mm(gate_ref[span, :], gate_grad_ref[...], NN) + mm(up_ref[span, :], up_grad_ref[...], NN)
+        back = mm(gate_ref[span, :], gate_grad_ref[...], NN) + mm(first_ref[span, :], up_grad_ref[:early, :], NN)
+        back += mm(rest_ref[span, :], up_grad_ref[early:, :], NN)
         back = back.T
         for part, value_ref in enumerate(value_refs):
             value_ref[:, span] = back[part * rows : (part + 1) * rows].astype(value_ref.dtype)
@@ -418,12 +430,14 @@
         ],
     )
     blocks = trade(blocks) if paired else [trade_whole(block, copies) for block in blocks]
-    (gate_here,) = call(
+    height = piece(inner)
+    early = max(1, inner // height * 2 // 3) * height
+    gate_here, up_first = call(
         fetch,
-        (places, in_hbm(w_gate[0])),
-        [SMEM, HBM],
-        [pltpu.VMEM((width, inner), bf16)],
-        [pltpu.SemaphoreType.DMA((1,))],
+        (places, in_hbm(w_gate[0]), in_hbm(w_up[0])),
+        [SMEM, HBM, HBM],
+        [pltpu.VMEM((width, inner), bf16), pltpu.VMEM((width, early), bf16)],
+        [pltpu.SemaphoreType.DMA((2,))],
         limit=1,
         flops=10**10,
         moved=2 * width * inner,
@@ -437,19 +451,18 @@
     else:
         inputs, grads = blocks[:1] + others[:1], blocks[1:] + others[1:]
     pieces = len(inputs)
-    height = piece(inner)
-    act, slope, silu, scaled, up_here = call(
+    act, slope, silu, scaled, up_rest = call(
         functools.partial(forward, pieces, paired),
-        (places, *inputs, gain_here, gate_here, in_hbm(w_up[0])),
-        [SMEM] + [VMEM] * (pieces + 2) + [HBM],
+        (places, *inputs, gain_here, gate_here, up_first, in_hbm(w_up[0])),
+        [SMEM] + [VMEM] * (pieces + 3) + [HBM],
         [
             shape((all_rows, inner), bf16),
             shape((inner, all_rows), f32),
             shape((inner, all_rows), f32),
             shape((all_rows, width), f32),
-            pltpu.VMEM((width, inner), bf16),
+            pltpu.VMEM((width, inner - early), bf16),
         ],
-        [pltpu.SemaphoreType.DMA((inner // height,))],
+        [pltpu.SemaphoreType.DMA(((inner - early) // height,))],
         limit=4,
         flops=4 * all_rows * width * inner,
         moved=4 * width * inner,
@@ -462,8 +475,8 @@
         value_shapes + [shape((inner, all_rows), bf16)] * 2,
         [
             pltpu.VMEM((all_rows, width), f32),
-            pltpu.VMEM((min(MIDDLE_FLIGHT + 1, inner // height), height, width), bf16),
-            pltpu.SemaphoreType.DMA((min(MIDDLE_FLIGHT + 1, inner // height),)),
+            pltpu.VMEM((min(4, inner // height), height, width), bf16),
+            pltpu.SemaphoreType.DMA((min(4, inner // height),)),
         ],
         limit=10,
         flops=4 * all_rows * width * inner,
@@ -471,8 +484,8 @@
     )
     *backs, gain_part = call(
         backward,
-        (gate_grad, up_grad, gate_here, up_here, scaled),
-        [VMEM] * 5,
+        (gate_grad, up_grad, gate_here, up_first, up_rest, scaled),
+        [VMEM] * 6,
         value_shapes + [shape((1, width), f32)],
         flops=4 * all_rows * width * inner,
         moved=4 * width * inner,

time: 79.3 us -> 79 us (level)
  waiting for transfers between devices: 21.3 us -> 20.5 us
  transfers between devices with their start and end apart: 20 -> 20, of which waited for: 8 -> 8; matrix products, arithmetic and copies ran while one was open for 0% -> 0% of each run, Pallas kernels for 18% -> 22%
where the time goes in v3:
time: 79 us; the launch traced here: 78.8 us
  Pallas kernels  36.4 us (46%)
  starting transfers between devices  21.2 us (27%)
  waiting for transfers between devices  20.5 us (26%)
    pallas_call x10, Pallas kernels, call(): pl.pallas_call(body, in_specs=in_specs, out_specs=[VMEM] * len(outs), out...  36.4 us
    ppermute x9, waiting for transfers between devices, trade(): lax.ppermute(blocks[step], 'expert', pairs[step])  17.1 us
    ppermute x9, starting transfers between devices, trade(): lax.ppermute(blocks[step], 'expert', pairs[step])  14.6 us
    ppermute x9, starting transfers between devices, swap(): return lax.ppermute(value, axis, [(i, i ^ 1) for i in range(size)])  4.25 us
    ppermute x1, waiting for transfers between devices, layer(): lax.ppermute(sums, ('dp', 'tensor'), [(i, i ^ 5) for i in range(8)])  2.76 us
    ppermute x1, starting transfers between devices, layer(): lax.ppermute(sums, ('dp', 'tensor'), [(i, i ^ 5) for i in range(8)])  1.81 us
  transfers between devices with their start and end apart: 20, of which 8 were waited for; matrix products, arithmetic and copies ran while one was open for 0% of the time, Pallas kernels for 22%

profile of v3, /device:TPU:0, one launch (start us, length us, event | category | flops | bytes accessed | tf_op | source)
XLA Modules:
  0.0 78.8 jit_solution(10472997977910380698)
XLA Ops:
  0.6 0.1 pad_add_fusion.places_ref
  0.7 2.0 %shard_map.120 = (bf16[16,3072]{1,0:T(8,128)(2,1)S(1)}, bf16[16,3072]{1,0:T(8,128)(2,1)S(1)}, bf16[16,3072]{1,0:T(8,128)(2,1)S(1)}, bf16[16,3072]{1,0:T(8,128)(2...) custom-call(s32[2]{0:T(128)S(1)} %pad_add_fusion.places_ref, ...), custom_call_target="tpu_custom_call" | custom-call | tf_op jit(solution)/shard_map/pallas_call | solution.py:30
  2.7 3.1 %collective-permute-start = (bf16[16,3072]{1,0:T(8,128)(2,1)S(1)}, bf16[16,3072]{1,0:T(8,128)(2,1)S(1)}, u32[]{:S(2)}, u32[]{:S(2)}) collective-permute-start(bf16[16,3072]{1,0:T(8,128)(2,1)S(1)} %get-tuple-element.59), channel_id=1, source_target_pairs={{0,2},{2,0},{4,6},{6,4},{1,3},{3,1},{5,7},{7,5},{8,10},{10,8},{12,... | collective-permute-start | bytes 294920 | tf_op jit(solution)/shard_map/ppermute | solution.py:383
  5.9 2.6 %collective-permute-start.1 = (bf16[16,3072]{1,0:T(8,128)(2,1)S(1)}, bf16[16,3072]{1,0:T(8,128)(2,1)S(1)}, u32[]{:S(2)}, u32[]{:S(2)}) collective-permute-start(bf16[16,3072]{1,0:T(8,128)(2,1)S(1)} %get-tuple-element.60), channel_id=1, source_target_pairs={{0,4},{2,6},{4,0},{6,2},{1,5},{3,7},{5,1},{7,3},{8,12},{10,14},{12... | collective-permute-start | bytes 294920 | tf_op jit(solution)/shard_map/ppermute | solution.py:383
  8.4 0.0 collective-permute-start.2
  8.5 0.0 collective-permute-start.3
  8.5 0.2 collective-permute-done.refs_1_
  8.7 0.3 collective-permute-start.4
  9.0 7.3 %collective-permute-done.1.refs_2_ = bf16[16,3072]{1,0:T(8,128)(2,1)S(1)} collective-permute-done((bf16[16,3072]{1,0:T(8,128)(2,1)S(1)}, bf16[16,3072]{1,0:T(8,128)(2,1)S(1)}, u32[]{:S(2)}, u32[]{:S(2)}) %collective-permute-start.1) | collective-permute-done | bytes 98336 | tf_op jit(solution)/shard_map/ppermute | solution.py:383
  16.3 0.0 collective-permute-start.5
  16.3 0.0 collective-permute-done.2.refs_3_
  16.3 0.5 collective-permute-start.6
  16.8 8.4 %shard_map.121 = (bf16[3072,2304]{1,0:T(8,128)(2,1)S(1)}, bf16[3072,1536]{1,0:T(8,128)(2,1)S(1)}) custom-call(s32[2]{0:T(128)S(1)} %pad_add_fusion.places_ref, bf16[3072,4608]{1,0:T(8,128)(2,1)} %bitcast.13, bf16[3072,4608]{1,0:T(8,128)(2,1)} %bitcast.11), custom_call_target="tpu_custom_call" | custom-call | flops 10000000000 | bytes 14155776 | tf_op jit(solution)/shard_map/pallas_call | solution.py:30
  25.2 0.0 collective-permute-done.3.refs_4_
  25.2 0.0 collective-permute-done.4.refs_5_
  25.3 0.0 collective-permute-done.5.refs_6_
  25.3 0.0 collective-permute-done.6.refs_7_
  25.3 6.8 %shard_map.122 = (bf16[64,2304]{1,0:T(8,128)(2,1)S(1)}, f32[2304,64]{1,0:T(8,128)S(1)}, f32[2304,64]{1,0:T(8,128)S(1)}, f32[64,3072]{1,0:T(8,128)S(1)}, bf16[3072,768]{1,0:T(8,128)(2,1)S(1)}) custom-call(s32[2]{0:T(128)S(1)} %pad_add_fusion.places_ref, bf16[16,3072]{1,0:T(8,128)(2,1)S(1)} %get-tuple-element.58.refs_0_, ...), custom_call_target="tpu_custom_call" | custom-call | flops 1811939328 | bytes 28311552 | tf_op jit(solution)/shard_map/pallas_call | solution.py:30
  32.1 8.5 %shard_map.123 = (f32[32,3072]{1,0:T(8,128)S(1)}, bf16[32,3072]{1,0:T(8,128)(2,1)S(1)}, bf16[2304,64]{1,0:T(8,128)(2,1)S(1)}, bf16[2304,64]{1,0:T(8,128)(2,1)S(1)}) custom-call(s32[2]{0:T(128)S(1)} %pad_add_fusion.places_ref, bf16[64,2304]{1,0:T(8,128)(2,1)S(1)} %get-tuple-element.65.act_ref, f32[2304,64]{1,0:T(8,128)S(1)} %get-tuple-element.66.slope_ref, ...), custom_call_target="tpu_custom_call" | custom-call | flops 1811939328 | bytes 14155776 | tf_op jit(solution)/shard_map/pallas_call | solution.py:30
  40.7 0.1 collective-permute-start.7
  40.8 8.0 %shard_map.124 = (f32[32,3072]{1,0:T(8,128)S(1)}, bf16[32,3072]{1,0:T(8,128)(2,1)S(1)}, f32[1,3072]{1,0:T(1,128)S(1)}) custom-call(bf16[2304,64]{1,0:T(8,128)(2,1)S(1)} %get-tuple-element.68.gate_grad_ref, bf16[2304,64]{1,0:T(8,128)(2,1)S(1)} %get-tuple-element.69.up_grad_ref, bf16[3072,2304]{1,0:T(8,128)(2,1)S(1)} %get-tuple-element.63.refs_9_.gate_ref, ...), custom_call_target="tpu_custom_call" | custom-call | flops 1811939328 | bytes 28311552 | tf_op jit(solution)/shard_map/pallas_call | solution.py:30
  48.7 0.6 collective-permute-start.12
  49.3 0.0 collective-permute-done.7.other_ref
  49.3 1.2 %collective-permute-start.8 = (bf16[8,3072]{1,0:T(8,128)(2,1)S(1)}, bf16[8,3072]{1,0:T(8,128)(2,1)S(1)}, u32[]{:S(2)}, u32[]{:S(2)}) collective-permute-start(bf16[8,3072]{1,0:T(8,128)(2,1)S(1)} %get-tuple-element.76), channel_id=1, source_target_pairs={{0,2},{2,0},{4,6},{6,4},{1,3},{3,1},{5,7},{7,5},{8,10},{10,8},{12,... | collective-permute-start | bytes 147464 | tf_op jit(solution)/shard_map/ppermute | solution.py:383
  50.5 1.9 %collective-permute-start.9 = (bf16[8,3072]{1,0:T(8,128)(2,1)S(1)}, bf16[8,3072]{1,0:T(8,128)(2,1)S(1)}, u32[]{:S(2)}, u32[]{:S(2)}) collective-permute-start(bf16[8,3072]{1,0:T(8,128)(2,1)S(1)} %get-tuple-element.77), channel_id=1, source_target_pairs={{0,4},{2,6},{4,0},{6,2},{1,5},{3,7},{5,1},{7,3},{8,12},{10,14},{12... | collective-permute-start | bytes 147464 | tf_op jit(solution)/shard_map/ppermute | solution.py:383
  52.4 1.3 %collective-permute-start.10 = (bf16[8,3072]{1,0:T(8,128)(2,1)S(1)}, bf16[8,3072]{1,0:T(8,128)(2,1)S(1)}, u32[]{:S(2)}, u32[]{:S(2)}) collective-permute-start(bf16[8,3072]{1,0:T(8,128)(2,1)S(1)} %get-tuple-element.78), channel_id=1, source_target_pairs={{0,6},{2,4},{4,2},{6,0},{1,7},{3,5},{5,3},{7,1},{8,14},{10,12},{12... | collective-permute-start | bytes 147464 | tf_op jit(solution)/shard_map/ppermute | solution.py:383
  53.8 0.0 collective-permute-done.8.refs_1_
  53.8 3.3 %collective-permute-done.9.refs_2_ = bf16[8,3072]{1,0:T(8,128)(2,1)S(1)} collective-permute-done((bf16[8,3072]{1,0:T(8,128)(2,1)S(1)}, bf16[8,3072]{1,0:T(8,128)(2,1)S(1)}, u32[]{:S(2)}, u32[]{:S(2)}) %collective-permute-start.9) | collective-permute-done | bytes 49184 | tf_op jit(solution)/shard_map/ppermute | solution.py:383
  57.1 1.3 %collective-permute-done.10.refs_3_ = bf16[8,3072]{1,0:T(8,128)(2,1)S(1)} collective-permute-done((bf16[8,3072]{1,0:T(8,128)(2,1)S(1)}, bf16[8,3072]{1,0:T(8,128)(2,1)S(1)}, u32[]{:S(2)}, u32[]{:S(2)}) %collective-permute-start.10) | collective-permute-done | bytes 49184 | tf_op jit(solution)/shard_map/ppermute | solution.py:383
  58.3 0.7 shard_map.126
  59.0 0.1 collective-permute-start.13
  59.1 1.6 %collective-permute-start.11 = (bf16[16,3200]{1,0:T(8,128)(2,1)S(1)}, bf16[16,3200]{1,0:T(8,128)(2,1)S(1)}, u32[]{:S(2)}, u32[]{:S(2)}) collective-permute-start(bf16[16,3200]{1,0:T(8,128)(2,1)S(1)} %get-tuple-element.79.mix_ref), channel_id=1, source_target_pairs={{0,1},{1,0},{2,3},{3,2},{4,5},{5,4},{6,7},{7,6},{8,9},{9,8},{10,11... | collective-permute-start | bytes 307208 | tf_op jit(solution)/shard_map/ppermute | solution.py:367
  60.6 0.0 collective-permute-done.12.other_ref
  60.6 0.0 collective-permute-done.13.other_sums_ref
  60.6 0.1 shard_map.127
  60.7 0.1 collective-permute-start.14
  60.8 2.3 %collective-permute-start.15 = (bf16[8,4992]{1,0:T(8,128)(2,1)S(1)}, bf16[8,4992]{1,0:T(8,128)(2,1)S(1)}, u32[]{:S(2)}, u32[]{:S(2)}) collective-permute-start(bf16[8,4992]{1,0:T(8,128)(2,1)S(1)} %get-tuple-element.85), channel_id=1, source_target_pairs={{0,4},{2,6},{4,0},{6,2},{1,5},{3,7},{5,1},{7,3},{8,12},{10,14},{12... | collective-permute-start | bytes 239624 | tf_op jit(solution)/shard_map/ppermute | solution.py:383
  63.1 2.1 %collective-permute-start.16 = (bf16[8,4992]{1,0:T(8,128)(2,1)S(1)}, bf16[8,4992]{1,0:T(8,128)(2,1)S(1)}, u32[]{:S(2)}, u32[]{:S(2)}) collective-permute-start(bf16[8,4992]{1,0:T(8,128)(2,1)S(1)} %get-tuple-element.86), channel_id=1, source_target_pairs={{0,6},{2,4},{4,2},{6,0},{1,7},{3,5},{5,3},{7,1},{8,14},{10,12},{12... | collective-permute-start | bytes 239624 | tf_op jit(solution)/shard_map/ppermute | solution.py:383
  65.2 0.0 collective-permute-done.11.other_mix_ref
  65.2 1.5 %collective-permute-done.14.refs_1_ = bf16[8,4992]{1,0:T(8,128)(2,1)S(1)} collective-permute-done((bf16[8,4992]{1,0:T(8,128)(2,1)S(1)}, bf16[8,4992]{1,0:T(8,128)(2,1)S(1)}, u32[]{:S(2)}, u32[]{:S(2)}) %collective-permute-start.14) | collective-permute-done | bytes 79904 | tf_op jit(solution)/shard_map/ppermute | solution.py:383
  66.6 3.5 %collective-permute-done.15.refs_2_ = bf16[8,4992]{1,0:T(8,128)(2,1)S(1)} collective-permute-done((bf16[8,4992]{1,0:T(8,128)(2,1)S(1)}, bf16[8,4992]{1,0:T(8,128)(2,1)S(1)}, u32[]{:S(2)}, u32[]{:S(2)}) %collective-permute-start.15) | collective-permute-done | bytes 79904 | tf_op jit(solution)/shard_map/ppermute | solution.py:383
  70.2 0.0 collective-permute-done.16.refs_3_
  70.2 0.8 %shard_map.128 = (bf16[16,4096]{1,0:T(8,128)(2,1)S(1)}, bf16[8,1920]{1,0:T(8,128)(2,1)S(1)}, bf16[16,3072]{1,0:T(8,128)(2,1)}, f32[16,128]{1,0:T(8,128)S(1)}) custom-call(bf16[32,16]{1,0:T(8,128)(2,1)S(1)} %get-tuple-element.49.first_ref, bf16[32,16]{1,0:T(8,128)(2,1)S(1)} %get-tuple-element.50.second_ref, ...), custom_call_target="tpu_custom_call" | custom-call | tf_op jit(solution)/shard_map/pallas_call | solution.py:30
  71.0 1.2 %collective-permute-start.17 = (bf16[16,4096]{1,0:T(8,128)(2,1)S(1)}, bf16[16,4096]{1,0:T(8,128)(2,1)S(1)}, u32[]{:S(2)}, u32[]{:S(2)}) collective-permute-start(bf16[16,4096]{1,0:T(8,128)(2,1)S(1)} %get-tuple-element.88.back_ref), channel_id=1, source_target_pairs={{0,1},{1,0},{2,3},{3,2},{4,5},{5,4},{6,7},{7,6},{8,9},{9,8},{10,11... | collective-permute-start | bytes 393224 | tf_op jit(solution)/shard_map/ppermute | solution.py:367
  72.2 1.8 %collective-permute-start.19 = (bf16[8,1920]{1,0:T(8,128)(2,1)S(1)}, bf16[8,1920]{1,0:T(8,128)(2,1)S(1)}, u32[]{:S(2)}, u32[]{:S(2)}) collective-permute-start(bf16[8,1920]{1,0:T(8,128)(2,1)S(1)} %get-tuple-element.90.refs_1_), channel_id=1, source_target_pairs={{0,17},{1,16},{8,25},{9,24},{16,1},{17,0},{24,9},{25,8},{2,19},{3,... | collective-permute-start | bytes 92168 | tf_op jit(solution)/shard_map/ppermute | solution.py:548
  74.0 0.5 collective-permute-start.18
  74.5 2.8 %collective-permute-done.19.refs_3_ = bf16[8,1920]{1,0:T(8,128)(2,1)S(1)} collective-permute-done((bf16[8,1920]{1,0:T(8,128)(2,1)S(1)}, bf16[8,1920]{1,0:T(8,128)(2,1)S(1)}, u32[]{:S(2)}, u32[]{:S(2)}) %collective-permute-start.19) | collective-permute-done | bytes 30752 | tf_op jit(solution)/shard_map/ppermute | solution.py:548
  77.2 0.6 collective-permute-done.18.refs_2_
  77.9 0.0 collective-permute-done.17.other_back_ref
  77.9 1.0 %shard_map.129 = (bf16[16,3072]{1,0:T(8,128)(2,1)}, f32[4,3072]{1,0:T(4,128)}, f32[1,3072]{1,0:T(1,128)}) custom-call(bf16[16,3072]{1,0:T(8,128)(2,1)S(1)} %get-tuple-element.51.tokens_ref, bf16[16,3072]{1,0:T(8,128)(2,1)S(1)} %get-tuple-element.56.cotangent_ref, f32[1,3072]{1,0:T(1,128)S(1)} %get-tuple-element.62.refs_8_.gain_ref, ...), custom_call_target="tpu_custom_call" | custom-call | tf_op jit(solution)/shard_map/pallas_call | solution.py:30
  (1 shorter events, 0.0 us)
Async XLA Ops:
  2.7 5.9 %collective-permute-start = (bf16[16,3072]{1,0:T(8,128)(2,1)S(1)}, bf16[16,3072]{1,0:T(8,128)(2,1)S(1)}, u32[]{:S(2)}, u32[]{:S(2)}) collective-permute-start(bf16[16,3072]{1,0:T(8,128)(2,1)S(1)} %get-tuple-element.59), channel_id=1, source_target_pairs={{0,2},{2,0},{4,6},{6,4},{1,3},{3,1},{5,7},{7,5},{8,10},{10,8},{12,... | collective-permute-start | bytes 294920 | tf_op jit(solution)/shard_map/ppermute | solution.py:383
  5.9 10.4 %collective-permute-start.1 = (bf16[16,3072]{1,0:T(8,128)(2,1)S(1)}, bf16[16,3072]{1,0:T(8,128)(2,1)S(1)}, u32[]{:S(2)}, u32[]{:S(2)}) collective-permute-start(bf16[16,3072]{1,0:T(8,128)(2,1)S(1)} %get-tuple-element.60), channel_id=1, source_target_pairs={{0,4},{2,6},{4,0},{6,2},{1,5},{3,7},{5,1},{7,3},{8,12},{10,14},{12... | collective-permute-start | bytes 294920 | tf_op jit(solution)/shard_map/ppermute | solution.py:383
  8.4 7.8 %collective-permute-start.2 = (bf16[16,3072]{1,0:T(8,128)(2,1)S(1)}, bf16[16,3072]{1,0:T(8,128)(2,1)S(1)}, u32[]{:S(2)}, u32[]{:S(2)}) collective-permute-start(bf16[16,3072]{1,0:T(8,128)(2,1)S(1)} %get-tuple-element.61), channel_id=1, source_target_pairs={{0,6},{2,4},{4,2},{6,0},{1,7},{3,5},{5,3},{7,1},{8,14},{10,12},{12... | collective-permute-start | bytes 294920 | tf_op jit(solution)/shard_map/ppermute | solution.py:383
  8.5 16.8 %collective-permute-start.3 = (bf16[16,3072]{1,0:T(8,128)(2,1)S(1)}, bf16[16,3072]{1,0:T(8,128)(2,1)S(1)}, u32[]{:S(2)}, u32[]{:S(2)}) collective-permute-start(bf16[16,3072]{1,0:T(8,128)(2,1)S(1)} %get-tuple-element.58.refs_0_), channel_id=1, source_target_pairs={{0,8},{8,0},{16,24},{24,16},{1,9},{9,1},{17,25},{25,17},{2,10},{10... | collective-permute-start | bytes 294920 | tf_op jit(solution)/shard_map/ppermute | solution.py:367
  8.7 16.6 %collective-permute-start.4 = (bf16[16,3072]{1,0:T(8,128)(2,1)S(1)}, bf16[16,3072]{1,0:T(8,128)(2,1)S(1)}, u32[]{:S(2)}, u32[]{:S(2)}) collective-permute-start(bf16[16,3072]{1,0:T(8,128)(2,1)S(1)} %collective-permute-done.refs_1_), channel_id=1, source_target_pairs={{0,8},{8,0},{16,24},{24,16},{1,9},{9,1},{17,25},{25,17},{2,10},{10... | collective-permute-start | bytes 294920 | tf_op jit(solution)/shard_map/ppermute | solution.py:367
  16.3 9.0 %collective-permute-start.5 = (bf16[16,3072]{1,0:T(8,128)(2,1)S(1)}, bf16[16,3072]{1,0:T(8,128)(2,1)S(1)}, u32[]{:S(2)}, u32[]{:S(2)}) collective-permute-start(bf16[16,3072]{1,0:T(8,128)(2,1)S(1)} %collective-permute-done.1.refs_2_), channel_id=1, source_target_pairs={{0,8},{8,0},{16,24},{24,16},{1,9},{9,1},{17,25},{25,17},{2,10},{10... | collective-permute-start | bytes 294920 | tf_op jit(solution)/shard_map/ppermute | solution.py:367
  16.3 9.0 %collective-permute-start.6 = (bf16[16,3072]{1,0:T(8,128)(2,1)S(1)}, bf16[16,3072]{1,0:T(8,128)(2,1)S(1)}, u32[]{:S(2)}, u32[]{:S(2)}) collective-permute-start(bf16[16,3072]{1,0:T(8,128)(2,1)S(1)} %collective-permute-done.2.refs_3_), channel_id=1, source_target_pairs={{0,8},{8,0},{16,24},{24,16},{1,9},{9,1},{17,25},{25,17},{2,10},{10... | collective-permute-start | bytes 294920 | tf_op jit(solution)/shard_map/ppermute | solution.py:367
  40.7 8.6 %collective-permute-start.7 = (bf16[32,3072]{1,0:T(8,128)(2,1)S(1)}, bf16[32,3072]{1,0:T(8,128)(2,1)S(1)}, u32[]{:S(2)}, u32[]{:S(2)}) collective-permute-start(bf16[32,3072]{1,0:T(8,128)(2,1)S(1)} %get-tuple-element.74), channel_id=1, source_target_pairs={{0,8},{8,0},{16,24},{24,16},{1,9},{9,1},{17,25},{25,17},{2,10},{10... | collective-permute-start | bytes 589832 | tf_op jit(solution)/shard_map/ppermute | solution.py:367
  48.7 11.9 %collective-permute-start.12 = (bf16[32,3072]{1,0:T(8,128)(2,1)S(1)}, bf16[32,3072]{1,0:T(8,128)(2,1)S(1)}, u32[]{:S(2)}, u32[]{:S(2)}) collective-permute-start(bf16[32,3072]{1,0:T(8,128)(2,1)S(1)} %get-tuple-element.81), channel_id=1, source_target_pairs={{0,8},{8,0},{16,24},{24,16},{1,9},{9,1},{17,25},{25,17},{2,10},{10... | collective-permute-start | bytes 589832 | tf_op jit(solution)/shard_map/ppermute | solution.py:367
  49.3 4.5 %collective-permute-start.8 = (bf16[8,3072]{1,0:T(8,128)(2,1)S(1)}, bf16[8,3072]{1,0:T(8,128)(2,1)S(1)}, u32[]{:S(2)}, u32[]{:S(2)}) collective-permute-start(bf16[8,3072]{1,0:T(8,128)(2,1)S(1)} %get-tuple-element.76), channel_id=1, source_target_pairs={{0,2},{2,0},{4,6},{6,4},{1,3},{3,1},{5,7},{7,5},{8,10},{10,8},{12,... | collective-permute-start | bytes 147464 | tf_op jit(solution)/shard_map/ppermute | solution.py:383
  50.5 6.6 %collective-permute-start.9 = (bf16[8,3072]{1,0:T(8,128)(2,1)S(1)}, bf16[8,3072]{1,0:T(8,128)(2,1)S(1)}, u32[]{:S(2)}, u32[]{:S(2)}) collective-permute-start(bf16[8,3072]{1,0:T(8,128)(2,1)S(1)} %get-tuple-element.77), channel_id=1, source_target_pairs={{0,4},{2,6},{4,0},{6,2},{1,5},{3,7},{5,1},{7,3},{8,12},{10,14},{12... | collective-permute-start | bytes 147464 | tf_op jit(solution)/shard_map/ppermute | solution.py:383
  52.4 5.9 %collective-permute-start.10 = (bf16[8,3072]{1,0:T(8,128)(2,1)S(1)}, bf16[8,3072]{1,0:T(8,128)(2,1)S(1)}, u32[]{:S(2)}, u32[]{:S(2)}) collective-permute-start(bf16[8,3072]{1,0:T(8,128)(2,1)S(1)} %get-tuple-element.78), channel_id=1, source_target_pairs={{0,6},{2,4},{4,2},{6,0},{1,7},{3,5},{5,3},{7,1},{8,14},{10,12},{12... | collective-permute-start | bytes 147464 | tf_op jit(solution)/shard_map/ppermute | solution.py:383
  59.0 1.6 %collective-permute-start.13 = (f32[8,1920]{1,0:T(8,128)S(1)}, f32[8,1920]{1,0:T(8,128)S(1)}, u32[]{:S(2)}, u32[]{:S(2)}) collective-permute-start(f32[8,1920]{1,0:T(8,128)S(1)} %get-tuple-element.82.sums_ref), channel_id=1, source_target_pairs={{0,8},{8,0},{16,24},{24,16},{1,9},{9,1},{17,25},{25,17},{2,10},{10... | collective-permute-start | bytes 184328 | tf_op jit(solution)/shard_map/ppermute | solution.py:367
  59.1 6.1 %collective-permute-start.11 = (bf16[16,3200]{1,0:T(8,128)(2,1)S(1)}, bf16[16,3200]{1,0:T(8,128)(2,1)S(1)}, u32[]{:S(2)}, u32[]{:S(2)}) collective-permute-start(bf16[16,3200]{1,0:T(8,128)(2,1)S(1)} %get-tuple-element.79.mix_ref), channel_id=1, source_target_pairs={{0,1},{1,0},{2,3},{3,2},{4,5},{5,4},{6,7},{7,6},{8,9},{9,8},{10,11... | collective-permute-start | bytes 307208 | tf_op jit(solution)/shard_map/ppermute | solution.py:367
  60.7 5.9 %collective-permute-start.14 = (bf16[8,4992]{1,0:T(8,128)(2,1)S(1)}, bf16[8,4992]{1,0:T(8,128)(2,1)S(1)}, u32[]{:S(2)}, u32[]{:S(2)}) collective-permute-start(bf16[8,4992]{1,0:T(8,128)(2,1)S(1)} %get-tuple-element.84), channel_id=1, source_target_pairs={{0,2},{2,0},{4,6},{6,4},{1,3},{3,1},{5,7},{7,5},{8,10},{10,8},{12,... | collective-permute-start | bytes 239624 | tf_op jit(solution)/shard_map/ppermute | solution.py:383
  60.8 9.3 %collective-permute-start.15 = (bf16[8,4992]{1,0:T(8,128)(2,1)S(1)}, bf16[8,4992]{1,0:T(8,128)(2,1)S(1)}, u32[]{:S(2)}, u32[]{:S(2)}) collective-permute-start(bf16[8,4992]{1,0:T(8,128)(2,1)S(1)} %get-tuple-element.85), channel_id=1, source_target_pairs={{0,4},{2,6},{4,0},{6,2},{1,5},{3,7},{5,1},{7,3},{8,12},{10,14},{12... | collective-permute-start | bytes 239624 | tf_op jit(solution)/shard_map/ppermute | solution.py:383
  63.1 7.1 %collective-permute-start.16 = (bf16[8,4992]{1,0:T(8,128)(2,1)S(1)}, bf16[8,4992]{1,0:T(8,128)(2,1)S(1)}, u32[]{:S(2)}, u32[]{:S(2)}) collective-permute-start(bf16[8,4992]{1,0:T(8,128)(2,1)S(1)} %get-tuple-element.86), channel_id=1, source_target_pairs={{0,6},{2,4},{4,2},{6,0},{1,7},{3,5},{5,3},{7,1},{8,14},{10,12},{12... | collective-permute-start | bytes 239624 | tf_op jit(solution)/shard_map/ppermute | solution.py:383
  71.0 6.9 %collective-permute-start.17 = (bf16[16,4096]{1,0:T(8,128)(2,1)S(1)}, bf16[16,4096]{1,0:T(8,128)(2,1)S(1)}, u32[]{:S(2)}, u32[]{:S(2)}) collective-permute-start(bf16[16,4096]{1,0:T(8,128)(2,1)S(1)} %get-tuple-element.88.back_ref), channel_id=1, source_target_pairs={{0,1},{1,0},{2,3},{3,2},{4,5},{5,4},{6,7},{7,6},{8,9},{9,8},{10,11... | collective-permute-start | bytes 393224 | tf_op jit(solution)/shard_map/ppermute | solution.py:367
  72.2 5.1 %collective-permute-start.19 = (bf16[8,1920]{1,0:T(8,128)(2,1)S(1)}, bf16[8,1920]{1,0:T(8,128)(2,1)S(1)}, u32[]{:S(2)}, u32[]{:S(2)}) collective-permute-start(bf16[8,1920]{1,0:T(8,128)(2,1)S(1)} %get-tuple-element.90.refs_1_), channel_id=1, source_target_pairs={{0,17},{1,16},{8,25},{9,24},{16,1},{17,0},{24,9},{25,8},{2,19},{3,... | collective-permute-start | bytes 92168 | tf_op jit(solution)/shard_map/ppermute | solution.py:548
  74.0 3.9 %collective-permute-start.18 = (bf16[8,1920]{1,0:T(8,128)(2,1)S(1)}, bf16[8,1920]{1,0:T(8,128)(2,1)S(1)}, u32[]{:S(2)}, u32[]{:S(2)}) collective-permute-start(bf16[8,1920]{1,0:T(8,128)(2,1)S(1)} %get-tuple-element.90.refs_1_), channel_id=1, source_target_pairs={{0,16},{8,24},{16,0},{24,8},{1,17},{9,25},{17,1},{25,9},{2,18},{10... | collective-permute-start | bytes 92168 | tf_op jit(solution)/shard_map/ppermute | solution.py:547
